TPU v7x, 256 devices: a whole 4x4x8 slice. The times are simulated.
256 devices in a mesh: seq: 128 (over z, x_hi, y, core), ch: 2 (over x_lo).
Axes of the slice: x: 4 (x_hi: 2, x_lo: 2; x = x_hi * 2 + x_lo), y: 4, z: 8, core: 2. Of those that a mesh axis runs over, the one named last changes fastest.
Arguments:
- query_gate: bfloat16 [2, 16384, 2048], P('ch', 'seq'), may hold values from -6 to 6
- key_input: bfloat16 [2, 16384, 2048], P('ch', 'seq'), may hold values from -6 to 6
- value_input: bfloat16 [2, 16384, 2048], P('ch', 'seq'), may hold values from -6 to 6
- grad_output: bfloat16 [2, 16384, 2048], P('ch', 'seq'), may hold values from -6 to 6
- filter_raw: bfloat16 [16384, 2048], P('seq'), may hold values from -6 to 6
- skip_gain: float32 [2048], replicated, may hold values from 0.5 to 1.5
Outputs:
- grad_query: bfloat16 [2, 16384, 2048], P('ch', 'seq')
- grad_key: bfloat16 [2, 16384, 2048], P('ch', 'seq')
- grad_value: bfloat16 [2, 16384, 2048], P('ch', 'seq')
- grad_filter: float32 [16384, 2048], P('seq', 'ch')
All inputs are finite; a program needn't handle non-finite values.
Results may differ from a plain program's by a relative error of at most 0.001.
Values sent between devices are 32-bit elements; how exact they have to be, the bound alone decides.
A program may use at most 128 MiB of HBM per device.

v0:
```python
import math

import jax
import jax.numpy as jnp
from jax import lax
from jax.sharding import PartitionSpec as P


def split_up(array, dim, size):
    shape = array.shape
    tiles = array.reshape(*shape[:dim], size, shape[dim] // size, *shape[dim + 1 :])
    return jnp.moveaxis(tiles, dim, 0)


def sent_and_summed(array, axis, dim):
    tiles = split_up(array, dim, lax.axis_size(axis))
    arrived = lax.all_to_all(tiles, axis, split_axis=0, concat_axis=0, tiled=True)
    return arrived.sum(axis=0)


def angle_table(row_index, col_index, modulus):
    turn_count = row_index[:, None] * col_index[None, :] % modulus
    angles = turn_count.astype(jnp.float32) * (2.0 * math.pi / modulus)
    return (jnp.cos(angles), jnp.sin(angles))


def contract(pattern, table, operand):
    return jnp.einsum(
        pattern, table, operand, precision=lax.Precision.HIGHEST, preferred_element_type=jnp.float32
    )


def rotate(pattern, cos_table, sin_table, sense_sign, real_part, imag_part, want_imag):
    if imag_part is None:
        cos_term = contract(pattern, cos_table, real_part)
        return (cos_term, sense_sign * contract(pattern, sin_table, real_part))
    real_out = contract(pattern, cos_table, real_part) - sense_sign * contract(
        pattern, sin_table, imag_part
    )
    if not want_imag:
        return (real_out, None)
    imag_out = contract(pattern, cos_table, imag_part) + sense_sign * contract(
        pattern, sin_table, real_part
    )
    return (real_out, imag_out)


def twist(cos_table, sin_table, sense_sign, real_part, imag_part):
    return (
        real_part * cos_table - sense_sign * imag_part * sin_table,
        imag_part * cos_table + sense_sign * real_part * sin_table,
    )


def spectral_terms(z_real, z_imag, g_real, g_imag, h_real, h_imag):
    conv_real = z_real * h_real - z_imag * h_imag
    conv_imag = z_real * h_imag + z_imag * h_real
    back_real = h_real * g_real + h_imag * g_imag
    back_imag = h_real * g_imag - h_imag * g_real
    corr_real = z_real * g_real + z_imag * g_imag
    corr_imag = z_real * g_imag - z_imag * g_real
    return (conv_real - back_imag, conv_imag + back_real, corr_real, corr_imag)


def shards(query_gate, key_input, value_input, grad_output, filter_raw, skip_gain):
    seq_count = lax.axis_size("seq")
    key_f = key_input[0].astype(jnp.float32)
    value_f = value_input[0].astype(jnp.float32)
    out_f = grad_output[0].astype(jnp.float32)
    mixed = key_f * value_f
    gated = out_f * query_gate[0].astype(jnp.float32)
    tokens, channels = mixed.shape
    seq_length = tokens * seq_count
    full_length = 2 * seq_length
    inverse_scale = 1.0 / full_length
    filter_taps = filter_raw.astype(jnp.float32) * seq_length ** (-0.5)
    freq_one = jnp.arange(2 * seq_count, dtype=jnp.int32)
    block_index = jnp.arange(seq_count, dtype=jnp.int32)
    offset_index = jnp.arange(tokens, dtype=jnp.int32)
    cos_one, sin_one = angle_table(freq_one, block_index, 2 * seq_count)
    cos_inv, sin_inv = angle_table(block_index, freq_one, 2 * seq_count)
    cos_two, sin_two = angle_table(offset_index, offset_index, tokens)
    local_width = channels // seq_count
    arrived = (
        lax.all_to_all(mixed.T, "seq", split_axis=0, concat_axis=1, tiled=True),
        lax.all_to_all(gated.T, "seq", split_axis=0, concat_axis=1, tiled=True),
        lax.all_to_all(filter_taps.T, "seq", split_axis=0, concat_axis=1, tiled=True),
    )
    cos_tw, sin_tw = angle_table(freq_one, offset_index, full_length)
    spectra = []
    for line_data in arrived:
        lines = line_data.reshape(local_width, seq_count, tokens)
        real_part, imag_part = rotate("kn,cnm->ckm", cos_one, sin_one, -1.0, lines, None, True)
        real_part, imag_part = twist(cos_tw, sin_tw, -1.0, real_part, imag_part)
        spectra.append(rotate("jm,ckm->ckj", cos_two, sin_two, -1.0, real_part, imag_part, True))
    packed_real, packed_imag, corr_real, corr_imag = spectral_terms(
        spectra[0][0], spectra[0][1], spectra[1][0], spectra[1][1], spectra[2][0], spectra[2][1]
    )
    pr_mid, pi_mid = rotate("mj,ckj->ckm", cos_two, sin_two, 1.0, packed_real, packed_imag, True)
    pr_mid, pi_mid = twist(cos_tw, sin_tw, 1.0, pr_mid, pi_mid)
    cr_mid, ci_mid = rotate("mj,ckj->ckm", cos_two, sin_two, 1.0, corr_real, corr_imag, True)
    cr_mid, ci_mid = twist(cos_tw, sin_tw, 1.0, cr_mid, ci_mid)
    conv_lines, back_lines = rotate("nk,ckm->cnm", cos_inv, sin_inv, 1.0, pr_mid, pi_mid, True)
    corr_lines = rotate("nk,ckm->cnm", cos_inv, sin_inv, 1.0, cr_mid, ci_mid, False)[0]
    conv_lines = (conv_lines * inverse_scale).reshape(local_width, seq_length)
    back_lines = (back_lines * inverse_scale).reshape(local_width, seq_length)
    corr_lines = (corr_lines * inverse_scale).reshape(local_width, seq_length)
    returned = (
        lax.all_to_all(conv_lines, "seq", split_axis=1, concat_axis=0, tiled=True),
        lax.all_to_all(back_lines, "seq", split_axis=1, concat_axis=0, tiled=True),
        lax.all_to_all(corr_lines, "seq", split_axis=1, concat_axis=0, tiled=True),
    )
    conv_time = returned[0].T
    back_time = returned[1].T
    corr_time = returned[2].T
    conv_full = conv_time + skip_gain * mixed
    back_full = back_time + skip_gain * gated
    grad_query = (out_f * conv_full).astype(jnp.bfloat16)[None]
    grad_key = (back_full * value_f).astype(jnp.bfloat16)[None]
    grad_value = (back_full * key_f).astype(jnp.bfloat16)[None]
    grad_filter = sent_and_summed(corr_time * seq_length ** (-0.5), "ch", 1)
    return (grad_query, grad_key, grad_value, grad_filter)


def solution(mesh):
    in_specs = (
        P("ch", "seq", None),
        P("ch", "seq", None),
        P("ch", "seq", None),
        P("ch", "seq", None),
        P("seq", None),
        P(),
    )
    out_specs = (P("ch", "seq", None), P("ch", "seq", None), P("ch", "seq", None), P("seq", "ch"))
    return jax.shard_map(shards, mesh=mesh, in_specs=in_specs, out_specs=out_specs, check_vma=False)
```

profile of v0, /device:TPU:32, one launch (start us, length us, event | category | flops | bytes accessed | tf_op | source)
XLA Modules:
  0.0 331.4 jit_solution(17355684770895490877)
XLA Ops:
  4.6 15.1 %all-to-all-start.2 = ((f32[128,16,128]{2,1,0:T(8,128)}), f32[128,16,128]{2,1,0:T(8,128)S(1)}, u32[]{:S(2)}, u32[]{:S(2)}) async-start(f32[128,16,128]{2,1,0:T(8,128)} %bitcast.20), calls=%async_computation.2 | async-start | bytes 2097152 | tf_op jit(solution)/shard_map/all_to_all | solution.py:86
  21.5 29.0 %all-to-all-done.2 = f32[128,16,128]{2,1,0:T(8,128)S(1)} async-done(((f32[128,16,128]{2,1,0:T(8,128)}), f32[128,16,128]{2,1,0:T(8,128)S(1)}, u32[]{:S(2)}, u32[]{:S(2)}) %all-to-all-start.2) | async-done | bytes 1048608 | tf_op jit(solution)/shard_map/all_to_all | solution.py:86
  50.5 6.7 %all-to-all-start = ((f32[128,16,128]{2,1,0:T(8,128)}), f32[128,16,128]{2,1,0:T(8,128)S(1)}, u32[]{:S(2)}, u32[]{:S(2)}) async-start(f32[128,16,128]{2,1,0:T(8,128)} %bitcast.239), calls=%async_computation | async-start | bytes 2097152 | tf_op jit(solution)/shard_map/all_to_all | solution.py:85
  59.6 28.4 %all-to-all-done = f32[128,16,128]{2,1,0:T(8,128)S(1)} async-done(((f32[128,16,128]{2,1,0:T(8,128)}), f32[128,16,128]{2,1,0:T(8,128)S(1)}, u32[]{:S(2)}, u32[]{:S(2)}) %all-to-all-start) | async-done | bytes 1048608 | tf_op jit(solution)/shard_map/all_to_all | solution.py:85
  88.1 7.4 %all-to-all-start.1 = ((f32[128,16,128]{2,1,0:T(8,128)}), f32[128,16,128]{2,1,0:T(8,128)}, u32[]{:S(2)}, u32[]{:S(2)}) async-start(f32[128,16,128]{2,1,0:T(8,128)} %bitcast.13), calls=%async_computation.1 | async-start | bytes 2097152 | tf_op jit(solution)/shard_map/all_to_all | solution.py:87
  101.6 3.6 %fusion.38 = f32[16,128,256]{2,1,0:T(8,128)S(1)} fusion(f32[128,16,128]{0,2,1:T(8,128)} %copy.75), kind=kOutput, calls=%fused_computation.69 | convolution fusion | flops 805765120 | bytes 3145728 | tf_op jit(solution)/shard_map/kn,cnm->ckm/dot_general | solution.py:28
  105.2 3.6 %fusion.40 = f32[16,128,256]{2,1,0:T(8,128)} fusion(f32[128,16,128]{0,2,1:T(8,128)S(1)} %copy-done.8), kind=kOutput, calls=%fused_computation.71 | convolution fusion | flops 805765120 | bytes 3145728 | tf_op jit(solution)/shard_map/kn,cnm->ckm/dot_general | solution.py:28
  108.8 3.6 %fusion.30 = f32[16,128,256]{2,1,0:T(8,128)} fusion(f32[128,16,128]{0,2,1:T(8,128)S(1)} %copy.91), kind=kOutput, calls=%fused_computation.61 | convolution fusion | flops 805765120 | bytes 3145728 | tf_op jit(solution)/shard_map/kn,cnm->ckm/dot_general | solution.py:28
  112.4 4.1 %fusion.32 = f32[16,128,256]{2,1,0:T(8,128)} fusion(f32[128,16,128]{0,2,1:T(8,128)S(1)} %copy.91), kind=kOutput, calls=%fused_computation.63 | convolution fusion | flops 805765120 | bytes 3145728 | tf_op jit(solution)/shard_map/kn,cnm->ckm/dot_general | solution.py:28
  116.5 9.2 %all-to-all-done.1 = f32[128,16,128]{2,1,0:T(8,128)} async-done(((f32[128,16,128]{2,1,0:T(8,128)}), f32[128,16,128]{2,1,0:T(8,128)}, u32[]{:S(2)}, u32[]{:S(2)}) %all-to-all-start.1) | async-done | bytes 1048608 | tf_op jit(solution)/shard_map/all_to_all | solution.py:87
  132.0 3.8 %fusion.54 = f32[16,256,128]{2,1,0:T(8,128)S(1)} fusion(f32[16,128,256]{2,1,0:T(8,128)S(1)} %fusion.34, f32[16,128,256]{2,1,0:T(8,128)S(1)} %fusion.36, f32[256,128]{0,1:T(8,128)S(1)} %copy-done.9, f32[256,128]{0,1:T(8,128)S(1)} %copy.79), kind=kOutput, calls=%fused_computation.82 | convolution fusion | flops 807108608 | bytes 6553600 | tf_op jit(solution)/shard_map/jm,ckm->ckj/dot_general | solution.py:28
  135.9 4.0 %fusion.58 = f32[16,256,128]{2,1,0:T(8,128)S(1)} fusion(f32[16,128,256]{2,1,0:T(8,128)S(1)} %fusion.34, f32[16,128,256]{2,1,0:T(8,128)S(1)} %fusion.36, f32[256,128]{0,1:T(8,128)S(1)} %copy.77, f32[256,128]{0,1:T(8,128)S(1)} %copy.76), kind=kOutput, calls=%fused_computation.83 | convolution fusion | flops 807108608 | bytes 6553600 | tf_op jit(solution)/shard_map/jm,ckm->ckj/dot_general | solution.py:28
  139.9 3.9 %fusion.60 = f32[16,256,128]{2,1,0:T(8,128)S(1)} fusion(f32[16,128,256]{2,1,0:T(8,128)S(1)} %copy-done.3, f32[16,128,256]{2,1,0:T(8,128)S(1)} %copy-done.4, f32[256,128]{0,1:T(8,128)S(1)} %copy.77, f32[256,128]{0,1:T(8,128)S(1)} %copy.76), kind=kOutput, calls=%fused_computation.84 | convolution fusion | flops 807108608 | bytes 6553600 | tf_op jit(solution)/shard_map/jm,ckm->ckj/dot_general | solution.py:28
  143.8 3.8 %fusion.64 = f32[16,256,128]{2,1,0:T(8,128)S(1)} fusion(f32[16,128,256]{2,1,0:T(8,128)S(1)} %copy-done.3, f32[16,128,256]{2,1,0:T(8,128)S(1)} %copy-done.4, f32[256,128]{0,1:T(8,128)S(1)} %copy-done.9, f32[256,128]{0,1:T(8,128)S(1)} %copy.79), kind=kOutput, calls=%fused_computation.85 | convolution fusion | flops 807108608 | bytes 6553600 | tf_op jit(solution)/shard_map/jm,ckm->ckj/dot_general | solution.py:28
  147.7 4.3 %fusion.48 = f32[16,256,128]{2,1,0:T(8,128)S(1)} fusion(f32[16,128,256]{2,1,0:T(8,128)S(1)} %fusion.38, f32[16,128,256]{2,1,0:T(8,128)S(1)} %copy-done.2, f32[256,128]{0,1:T(8,128)S(1)} %copy-done.9, f32[256,128]{0,1:T(8,128)S(1)} %copy.79), kind=kOutput, calls=%fused_computation.80 | convolution fusion | flops 807108608 | bytes 6553600 | tf_op jit(solution)/shard_map/jm,ckm->ckj/dot_general | solution.py:28
  151.9 3.9 %fusion.52 = f32[16,256,128]{2,1,0:T(8,128)S(1)} fusion(f32[16,128,256]{2,1,0:T(8,128)S(1)} %fusion.38, f32[16,128,256]{2,1,0:T(8,128)S(1)} %copy-done.2, f32[256,128]{0,1:T(8,128)S(1)} %copy.77, f32[256,128]{0,1:T(8,128)S(1)} %copy.76), kind=kOutput, calls=%fused_computation.81 | convolution fusion | flops 807108608 | bytes 6553600 | tf_op jit(solution)/shard_map/jm,ckm->ckj/dot_general | solution.py:28
  155.8 3.9 %multiply_add_fusion.3 = f32[16,256,128]{2,1,0:T(8,128)S(1)} fusion(f32[16,256,128]{2,1,0:T(8,128)S(1)} %fusion.54, f32[16,128,256]{2,1,0:T(8,128)S(1)} %fusion.34, f32[16,128,256]{2,1,0:T(8,128)S(1)} %fusion.36, f32[256,128]{0,1:T(8,128)S(1)} %copy.77, f32[256,128]{0,1:T(8,128)S(1)} %copy.76), kind=kOutput, calls=%fused_computation.34 | convolution fusion | flops 808157184 | bytes 8650752 | tf_op jit(solution)/shard_map/jm,ckm->ckj/dot_general | solution.py:28
  159.8 3.9 %multiply_subtract_fusion.3 = f32[16,256,128]{2,1,0:T(8,128)S(1)} fusion(f32[16,256,128]{2,1,0:T(8,128)S(1)} %fusion.58, f32[16,128,256]{2,1,0:T(8,128)S(1)} %fusion.34, f32[16,128,256]{2,1,0:T(8,128)S(1)} %fusion.36, f32[256,128]{0,1:T(8,128)S(1)} %copy-done.9, f32[256,128]{0,1:T(8,128)S(1)} %copy.79), kind=kOutput, calls=%fused_computation.36 | convolution fusion | flops 808157184 | bytes 8650752 | tf_op jit(solution)/shard_map/jm,ckm->ckj/dot_general | solution.py:28
  163.7 4.1 %multiply_subtract_fusion.2 = f32[16,256,128]{2,1,0:T(8,128)S(1)} fusion(f32[16,256,128]{2,1,0:T(8,128)S(1)} %fusion.60, f32[16,128,256]{2,1,0:T(8,128)S(1)} %copy-done.3, f32[16,128,256]{2,1,0:T(8,128)S(1)} %copy-done.4, f32[256,128]{0,1:T(8,128)S(1)} %copy-done.9, f32[256,128]{0,1:T(8,128)S(1)} %copy.79), kind=kOutput, calls=%fused_computation.32 | convolution fusion | flops 808157184 | bytes 8650752 | tf_op jit(solution)/shard_map/jm,ckm->ckj/dot_general | solution.py:28
  167.8 3.9 %multiply_add_fusion.2 = f32[16,256,128]{2,1,0:T(8,128)S(1)} fusion(f32[16,256,128]{2,1,0:T(8,128)S(1)} %fusion.64, f32[16,128,256]{2,1,0:T(8,128)S(1)} %copy-done.3, f32[16,128,256]{2,1,0:T(8,128)S(1)} %copy-done.4, f32[256,128]{0,1:T(8,128)S(1)} %copy.77, f32[256,128]{0,1:T(8,128)S(1)} %copy.76), kind=kOutput, calls=%fused_computation.33 | convolution fusion | flops 808157184 | bytes 8650752 | tf_op jit(solution)/shard_map/jm,ckm->ckj/dot_general | solution.py:28
  171.7 3.9 %multiply_subtract_fusion.4 = f32[16,256,128]{2,1,0:T(8,128)S(1)} fusion(f32[16,256,128]{2,1,0:T(8,128)S(1)} %fusion.52, f32[16,128,256]{2,1,0:T(8,128)S(1)} %fusion.38, f32[16,128,256]{2,1,0:T(8,128)S(1)} %copy-done.2, f32[256,128]{0,1:T(8,128)S(1)} %copy-done.9, f32[256,128]{0,1:T(8,128)S(1)} %copy.79), kind=kOutput, calls=%fused_computation.37 | convolution fusion | flops 808157184 | bytes 8650752 | tf_op jit(solution)/shard_map/jm,ckm->ckj/dot_general | solution.py:28
  175.6 7.0 %multiply_subtract_fusion = (f32[16,256,128]{2,1,0:T(8,128)S(1)}, f32[16,256,128]{2,1,0:T(8,128)S(1)}, f32[16,256,128]{2,1,0:T(8,128)}, f32[16,256,128]{2,1,0:T(8,128)}) fusion(f32[16,256,128]{2,1,0:T(8,128)S(1)} %multiply_subtract_fusion.2, f32[16,256,128]{2,1,0:T(8,128)S(1)} %multiply_subtract_fusion.4, f32[16,256,128]{2,1,0:T(8,128)S(1)} %multiply_add_fusion.2, ...), kind=kOutput, calls=%fused_computation.26 | convolution fusion | flops 818642944 | bytes 25427968 | tf_op jit(solution)/shard_map/jm,ckm->ckj/dot_general | solution.py:28
  198.1 7.2 %all-to-all-start.5 = ((f32[16,128,128]{2,0,1:T(8,128)}), f32[16,128,128]{2,0,1:T(8,128)}, u32[]{:S(2)}, u32[]{:S(2)}) async-start(f32[16,128,128]{2,0,1:T(8,128)} %copy.106), calls=%async_computation.5 | async-start | bytes 2097152 | tf_op jit(solution)/shard_map/all_to_all | solution.py:111
  220.9 14.8 %all-to-all-done.5 = f32[16,128,128]{2,0,1:T(8,128)} async-done(((f32[16,128,128]{2,0,1:T(8,128)}), f32[16,128,128]{2,0,1:T(8,128)}, u32[]{:S(2)}, u32[]{:S(2)}) %all-to-all-start.5) | async-done | bytes 1048608 | tf_op jit(solution)/shard_map/all_to_all | solution.py:111
  235.7 7.2 %all-to-all-start.4 = ((f32[16,128,128]{2,0,1:T(8,128)}), f32[16,128,128]{2,0,1:T(8,128)}, u32[]{:S(2)}, u32[]{:S(2)}) async-start(f32[16,128,128]{2,0,1:T(8,128)} %copy.101), calls=%async_computation.4 | async-start | bytes 2097152 | tf_op jit(solution)/shard_map/all_to_all | solution.py:110
  243.0 4.1 %fusion.46 = f32[16,128,128]{2,1,0:T(8,128)S(1)} fusion(f32[16,256,128]{1,2,0:T(8,128)S(1)} %convolution_add_fusion.1, f32[16,256,128]{1,2,0:T(8,128)} %copy-done, f32[256,128]{0,1:T(8,128)S(1)} %copy.77, f32[256,128]{0,1:T(8,128)S(1)} %copy.76), kind=kOutput, calls=%fused_computation.78 | convolution fusion | flops 807337984 | bytes 5505024 | tf_op jit(solution)/shard_map/nk,ckm->cnm/dot_general | solution.py:28
  250.9 22.5 %all-to-all-done.4 = f32[16,128,128]{2,0,1:T(8,128)} async-done(((f32[16,128,128]{2,0,1:T(8,128)}), f32[16,128,128]{2,0,1:T(8,128)}, u32[]{:S(2)}, u32[]{:S(2)}) %all-to-all-start.4) | async-done | bytes 1048608 | tf_op jit(solution)/shard_map/all_to_all | solution.py:110
  273.4 6.7 %all-to-all-start.3 = ((f32[16,128,128]{2,0,1:T(8,128)}), f32[16,128,128]{2,0,1:T(8,128)S(1)}, u32[]{:S(2)}, u32[]{:S(2)}) async-start(f32[16,128,128]{2,0,1:T(8,128)} %copy.100), calls=%async_computation.3 | async-start | bytes 2097152 | tf_op jit(solution)/shard_map/all_to_all | solution.py:109
  282.6 28.3 %all-to-all-done.3 = f32[16,128,128]{2,0,1:T(8,128)S(1)} async-done(((f32[16,128,128]{2,0,1:T(8,128)}), f32[16,128,128]{2,0,1:T(8,128)S(1)}, u32[]{:S(2)}, u32[]{:S(2)}) %all-to-all-start.3) | async-done | bytes 1048608 | tf_op jit(solution)/shard_map/all_to_all | solution.py:109
  311.9 3.6 %all-to-all-start.6 = ((f32[2,128,1024]{1,2,0:T(8,128)}), f32[2,128,1024]{1,2,0:T(8,128)S(1)}, u32[]{:S(2)}, u32[]{:S(2)}) async-start(f32[2,128,1024]{1,2,0:T(8,128)} %bitcast.44), calls=%async_computation.6 | async-start | bytes 2097152 | tf_op jit(solution)/shard_map/all_to_all | solution.py:17
  315.5 3.3 fusion.66
  323.9 6.0 %all-to-all-done.6 = f32[2,128,1024]{1,2,0:T(8,128)S(1)} async-done(((f32[2,128,1024]{1,2,0:T(8,128)}), f32[2,128,1024]{1,2,0:T(8,128)S(1)}, u32[]{:S(2)}, u32[]{:S(2)}) %all-to-all-start.6) | async-done | bytes 1048608 | tf_op jit(solution)/shard_map/all_to_all | solution.py:17
  (91 shorter events, 64.8 us)
Async XLA Ops:
  1.9 2.6 copy-start.10
  3.5 1.1 copy-start.12
  3.5 16.3 %copy-start.21 = (bf16[1,128,2048]{2,1,0:T(8,128)(2,1)S(1)}, bf16[1,128,2048]{2,1,0:T(8,128)(2,1)}, u32[]{:S(2)}) copy-start(bf16[1,128,2048]{2,1,0:T(8,128)(2,1)} %param.7) | copy-start | bytes 1572868
  4.6 15.5 %copy-start.22 = (bf16[1,128,2048]{2,1,0:T(8,128)(2,1)S(1)}, bf16[1,128,2048]{2,1,0:T(8,128)(2,1)}, u32[]{:S(2)}) copy-start(bf16[1,128,2048]{2,1,0:T(8,128)(2,1)} %param.8) | copy-start | bytes 1572868
  4.6 45.9 %all-to-all-start.2 = ((f32[128,16,128]{2,1,0:T(8,128)}), f32[128,16,128]{2,1,0:T(8,128)S(1)}, u32[]{:S(2)}, u32[]{:S(2)}) async-start(f32[128,16,128]{2,1,0:T(8,128)} %bitcast.20), calls=%async_computation.2 | async-start | bytes 2097152 | tf_op jit(solution)/shard_map/all_to_all | solution.py:86
  20.1 30.5 %copy-start.14 = (bf16[1,128,2048]{1,2,0:T(8,128)(2,1)}, bf16[1,128,2048]{1,2,0:T(8,128)(2,1)S(1)}, u32[]{:S(2)}) copy-start(bf16[1,128,2048]{1,2,0:T(8,128)(2,1)S(1)} %copy.73) | copy-start | bytes 1572868
  20.3 30.2 %copy-start.16 = (bf16[1,128,2048]{1,2,0:T(8,128)(2,1)}, bf16[1,128,2048]{1,2,0:T(8,128)(2,1)S(1)}, u32[]{:S(2)}) copy-start(bf16[1,128,2048]{1,2,0:T(8,128)(2,1)S(1)} %copy.74) | copy-start | bytes 1572868
  50.5 37.5 %all-to-all-start = ((f32[128,16,128]{2,1,0:T(8,128)}), f32[128,16,128]{2,1,0:T(8,128)S(1)}, u32[]{:S(2)}, u32[]{:S(2)}) async-start(f32[128,16,128]{2,1,0:T(8,128)} %bitcast.239), calls=%async_computation | async-start | bytes 2097152 | tf_op jit(solution)/shard_map/all_to_all | solution.py:85
  88.1 9.8 %copy-start.18 = (f32[128,16,128]{2,1,0:T(8,128)}, f32[128,16,128]{2,1,0:T(8,128)S(1)}, u32[]{:S(2)}) copy-start(f32[128,16,128]{2,1,0:T(8,128)S(1)} %all-to-all-done) | copy-start | bytes 3145732
  88.1 37.7 %all-to-all-start.1 = ((f32[128,16,128]{2,1,0:T(8,128)}), f32[128,16,128]{2,1,0:T(8,128)}, u32[]{:S(2)}, u32[]{:S(2)}) async-start(f32[128,16,128]{2,1,0:T(8,128)} %bitcast.13), calls=%async_computation.1 | async-start | bytes 2097152 | tf_op jit(solution)/shard_map/all_to_all | solution.py:87
  101.6 3.6 %copy-start.8 = (f32[128,16,128]{0,2,1:T(8,128)S(1)}, f32[128,16,128]{0,2,1:T(8,128)}, u32[]{:S(2)}) copy-start(f32[128,16,128]{0,2,1:T(8,128)} %copy.75) | copy-start | bytes 3145732
  129.7 2.4 copy-start.9
  135.9 4.1 %copy-start.3 = (f32[16,128,256]{2,1,0:T(8,128)S(1)}, f32[16,128,256]{2,1,0:T(8,128)}, u32[]{:S(2)}) copy-start(f32[16,128,256]{2,1,0:T(8,128)} %fusion.30) | copy-start | bytes 6291460
  135.9 4.1 %copy-start.4 = (f32[16,128,256]{2,1,0:T(8,128)S(1)}, f32[16,128,256]{2,1,0:T(8,128)}, u32[]{:S(2)}) copy-start(f32[16,128,256]{2,1,0:T(8,128)} %fusion.32) | copy-start | bytes 6291460
  143.8 3.8 %copy-start.2 = (f32[16,128,256]{2,1,0:T(8,128)S(1)}, f32[16,128,256]{2,1,0:T(8,128)}, u32[]{:S(2)}) copy-start(f32[16,128,256]{2,1,0:T(8,128)} %fusion.40) | copy-start | bytes 6291460
  196.7 8.6 %copy-start.5 = (f32[16,256,128]{2,1,0:T(8,128)S(1)}, f32[16,256,128]{2,1,0:T(8,128)}, u32[]{:S(2)}) copy-start(f32[16,256,128]{2,1,0:T(8,128)} %get-tuple-element.16) | copy-start | bytes 6291460
  198.1 37.6 %all-to-all-start.5 = ((f32[16,128,128]{2,0,1:T(8,128)}), f32[16,128,128]{2,0,1:T(8,128)}, u32[]{:S(2)}, u32[]{:S(2)}) async-start(f32[16,128,128]{2,0,1:T(8,128)} %copy.106), calls=%async_computation.5 | async-start | bytes 2097152 | tf_op jit(solution)/shard_map/all_to_all | solution.py:111
  205.3 2.2 copy-start.7
  209.8 2.4 copy-start.6
  214.5 2.4 copy-start
  235.7 37.7 %all-to-all-start.4 = ((f32[16,128,128]{2,0,1:T(8,128)}), f32[16,128,128]{2,0,1:T(8,128)}, u32[]{:S(2)}, u32[]{:S(2)}) async-start(f32[16,128,128]{2,0,1:T(8,128)} %copy.101), calls=%async_computation.4 | async-start | bytes 2097152 | tf_op jit(solution)/shard_map/all_to_all | solution.py:110
  242.9 4.1 %copy-start.1 = (f32[16,256,128]{1,2,0:T(8,128)S(1)}, f32[16,256,128]{1,2,0:T(8,128)}, u32[]{:S(2)}) copy-start(f32[16,256,128]{1,2,0:T(8,128)} %copy-done) | copy-start | bytes 6291460
  273.4 37.5 %all-to-all-start.3 = ((f32[16,128,128]{2,0,1:T(8,128)}), f32[16,128,128]{2,0,1:T(8,128)S(1)}, u32[]{:S(2)}, u32[]{:S(2)}) async-start(f32[16,128,128]{2,0,1:T(8,128)} %copy.100), calls=%async_computation.3 | async-start | bytes 2097152 | tf_op jit(solution)/shard_map/all_to_all | solution.py:109
  280.1 35.3 %copy-start.11 = (bf16[1,128,2048]{1,2,0:T(8,128)(2,1)S(1)}, bf16[1,128,2048]{1,2,0:T(8,128)(2,1)}, u32[]{:S(2)}) copy-start(bf16[1,128,2048]{1,2,0:T(8,128)(2,1)} %copy-done.10) | copy-start | bytes 1572868
  280.1 35.3 %copy-start.13 = (bf16[1,128,2048]{1,2,0:T(8,128)(2,1)S(1)}, bf16[1,128,2048]{1,2,0:T(8,128)(2,1)}, u32[]{:S(2)}) copy-start(bf16[1,128,2048]{1,2,0:T(8,128)(2,1)} %copy-done.12) | copy-start | bytes 1572868
  280.2 35.3 %copy-start.15 = (bf16[1,128,2048]{1,2,0:T(8,128)(2,1)S(1)}, bf16[1,128,2048]{1,2,0:T(8,128)(2,1)}, u32[]{:S(2)}) copy-start(bf16[1,128,2048]{1,2,0:T(8,128)(2,1)} %copy-done.14) | copy-start | bytes 1572868
  280.2 35.3 %copy-start.17 = (bf16[1,128,2048]{1,2,0:T(8,128)(2,1)S(1)}, bf16[1,128,2048]{1,2,0:T(8,128)(2,1)}, u32[]{:S(2)}) copy-start(bf16[1,128,2048]{1,2,0:T(8,128)(2,1)} %copy-done.16) | copy-start | bytes 1572868
  280.2 35.3 %copy-start.23 = (f32[2048]{0:T(1024)S(1)}, f32[2048]{0:T(1024)}, u32[]{:S(2)}) copy-start(f32[2048]{0:T(1024)} %param.11) | copy-start | bytes 24580
  310.9 1.0 copy-start.19
  311.9 18.1 %all-to-all-start.6 = ((f32[2,128,1024]{1,2,0:T(8,128)}), f32[2,128,1024]{1,2,0:T(8,128)S(1)}, u32[]{:S(2)}, u32[]{:S(2)}) async-start(f32[2,128,1024]{1,2,0:T(8,128)} %bitcast.44), calls=%async_computation.6 | async-start | bytes 2097152 | tf_op jit(solution)/shard_map/all_to_all | solution.py:17
  318.8 4.1 %copy-start.20 = (bf16[128,2048]{0,1:T(8,128)(2,1)S(1)}, bf16[128,2048]{0,1:T(8,128)(2,1)}, u32[]{:S(2)}) copy-start(bf16[128,2048]{0,1:T(8,128)(2,1)} %get-tuple-element.20) | copy-start | bytes 1572868
where the time goes:
time: 338 us; the launch traced here: 331 us
  waiting for transfers between devices  138 us (41%)
  matrix products  105 us (31%)
  starting transfers between devices  54.1 us (16%)
  local copies, waits for them, and re-layouts  21.7 us (6%)
  other arithmetic  11 us (3%)
    dot_general x32, matrix products, contract(): jnp.einsum(pattern, table, operand, precision=lax.Precision.HIGHEST, pref...  105 us
    all_to_all x1, waiting for transfers between devices, shards(): lax.all_to_all(gated.T, 'seq', split_axis=0, concat_axis=1, tiled=True)  29 us
    all_to_all x1, waiting for transfers between devices, shards(): lax.all_to_all(mixed.T, 'seq', split_axis=0, concat_axis=1, tiled=True)  28.4 us
    all_to_all x1, waiting for transfers between devices, shards(): lax.all_to_all(conv_lines, 'seq', split_axis=1, concat_axis=0, tiled=True)  28.3 us
    all_to_all x1, waiting for transfers between devices, shards(): lax.all_to_all(back_lines, 'seq', split_axis=1, concat_axis=0, tiled=True)  22.5 us
    all_to_all x1, starting transfers between devices, shards(): lax.all_to_all(gated.T, 'seq', split_axis=0, concat_axis=1, tiled=True)  15.1 us
    all_to_all x1, waiting for transfers between devices, shards(): lax.all_to_all(corr_lines, 'seq', split_axis=1, concat_axis=0, tiled=True)  14.8 us
    unnamed x57, local copies, waits for them, and re-layouts  11.9 us
  transfers between devices with their start and end apart: 7, of which 7 were waited for; matrix products, arithmetic and copies ran while one was open for 18% of the time, Pallas kernels for 0%

commit v1 on v0

v1 whole, which is shorter than its diff:
```python
import functools
import math

import jax
import jax.numpy as jnp
import numpy as np
from jax import lax
from jax.experimental import pallas as pl
from jax.experimental.pallas import tpu as pltpu
from jax.sharding import PartitionSpec as P

BLOCK = 128
FULL = 2 * BLOCK * BLOCK
F32 = jnp.float32
BF16 = jnp.bfloat16


def split_table(table):
    high = jnp.asarray(table, F32).astype(BF16)
    low = (jnp.asarray(table, F32) - high.astype(F32)).astype(BF16)
    return (high, low)


def tables():
    idx = np.arange(BLOCK)
    turn_one = 2.0 * math.pi / (2 * BLOCK) * ((idx[:, None] + 0.5) * idx[None, :])
    first = np.concatenate([np.cos(turn_one), -np.sin(turn_one)], axis=0)
    turn_two = 2.0 * math.pi / BLOCK * (idx[:, None] * idx[None, :] % BLOCK)
    cos_two, sin_two = np.cos(turn_two), np.sin(turn_two)
    second = np.block([[cos_two, -sin_two], [sin_two, cos_two]])
    second_inv = np.block([[cos_two, sin_two], [-sin_two, cos_two]])
    turn_mid = 2.0 * math.pi / FULL * ((idx[:, None] + 0.5) * idx[None, :])
    out = []
    for table in (first, second, second_inv, first.T):
        out.extend(split_table(table.astype(np.float32)))
    out.append(jnp.asarray(np.cos(turn_mid), F32))
    out.append(jnp.asarray(np.sin(turn_mid), F32))
    return tuple(out)


def halves(x):
    high = x.astype(BF16)
    return (high, (x - high.astype(F32)).astype(BF16))


def dot(a, b):
    return jnp.dot(a, b, preferred_element_type=F32)


def dot_left(high, low, x):
    x_high, x_low = halves(x)
    return dot(high, x_high) + dot(low, x_high) + dot(high, x_low)


def dot_right(x, high, low):
    x_high, x_low = halves(x)
    return dot(x_high, high) + dot(x_high, low) + dot(x_low, high)


def to_spectrum(parts, tab):
    f_high, f_low, s_high, s_low = tab[0][...], tab[1][...], tab[2][...], tab[3][...]
    cos_mid, sin_mid = tab[8][...], tab[9][...]
    lines = dot_left(f_high, f_low, jnp.concatenate(parts, axis=1))
    rows = []
    for i in range(len(parts)):
        re = lines[:BLOCK, i * BLOCK : (i + 1) * BLOCK]
        im = lines[BLOCK:, i * BLOCK : (i + 1) * BLOCK]
        rows.append(
            jnp.concatenate([re * cos_mid + im * sin_mid, im * cos_mid - re * sin_mid], axis=1)
        )
    spec = dot_right(jnp.concatenate(rows, axis=0), s_high, s_low)
    return [
        (spec[i * BLOCK : (i + 1) * BLOCK, :BLOCK], spec[i * BLOCK : (i + 1) * BLOCK, BLOCK:])
        for i in range(len(parts))
    ]


def from_spectrum(specs, tab):
    i_high, i_low, t_high, t_low = tab[4][...], tab[5][...], tab[6][...], tab[7][...]
    cos_mid, sin_mid = tab[8][...], tab[9][...]
    rows = jnp.concatenate([jnp.concatenate([re, im], axis=1) for re, im in specs], axis=0)
    mid = dot_right(rows, i_high, i_low)
    cols = []
    for i in range(len(specs)):
        re = mid[i * BLOCK : (i + 1) * BLOCK, :BLOCK]
        im = mid[i * BLOCK : (i + 1) * BLOCK, BLOCK:]
        cols.append(
            jnp.concatenate([re * cos_mid - im * sin_mid, im * cos_mid + re * sin_mid], axis=0)
        )
    lines = dot_left(t_high, t_low, jnp.concatenate(cols, axis=1))
    return [lines[:, i * BLOCK : (i + 1) * BLOCK] for i in range(len(specs))]


SCALE = 1.0 / (BLOCK * (FULL // 2))


def channel_rows(part, channel):
    return pl.ds(part * BLOCK * 8 + channel, BLOCK, stride=8)


def conv_kernel(*refs):
    tab, (mixed_ref, taps_ref, conv_ref, mspec_ref, tspec_ref) = refs[:10], refs[10:]

    def body(c, carry):
        parts = [mixed_ref[channel_rows(b, c), :] for b in range(2)]
        parts.append(taps_ref[channel_rows(0, c), :])
        mixed_a, mixed_b, taps = to_spectrum(parts, tab)
        prods = []
        for b, (re, im) in enumerate((mixed_a, mixed_b)):
            mspec_ref[c, b, 0] = re
            mspec_ref[c, b, 1] = im
            prods.append((re * taps[0] - im * taps[1], re * taps[1] + im * taps[0]))
        tspec_ref[c, 0] = taps[0]
        tspec_ref[c, 1] = taps[1]
        lines = from_spectrum(prods, tab)
        for b in range(2):
            conv_ref[channel_rows(b, c), :] = lines[b] * SCALE
        return carry

    lax.fori_loop(0, 8, body, 0)


def back_kernel(*refs):
    tab, (gated_ref, mspec_ref, tspec_ref, back_ref, corr_ref) = refs[:10], refs[10:]

    def body(c, carry):
        gated = to_spectrum([gated_ref[channel_rows(b, c), :] for b in range(2)], tab)
        t_re, t_im = tspec_ref[c, 0], tspec_ref[c, 1]
        prods = []
        corr_re = corr_im = None
        for b, (re, im) in enumerate(gated):
            m_re, m_im = mspec_ref[c, b, 0], mspec_ref[c, b, 1]
            prods.append((t_re * re + t_im * im, t_re * im - t_im * re))
            term_re = m_re * re + m_im * im
            term_im = m_re * im - m_im * re
            corr_re = term_re if corr_re is None else corr_re + term_re
            corr_im = term_im if corr_im is None else corr_im + term_im
        prods.append((corr_re, corr_im))
        lines = from_spectrum(prods, tab)
        for b in range(2):
            back_ref[channel_rows(b, c), :] = lines[b] * SCALE
        corr_ref[channel_rows(0, c), :] = lines[2] * SCALE
        return carry

    lax.fori_loop(0, 8, body, 0)


def call(kernel, out_shapes, operands, name):
    vmem = pl.BlockSpec(memory_space=pltpu.VMEM)
    return pl.pallas_call(
        kernel,
        out_shape=[jax.ShapeDtypeStruct(s, F32) for s in out_shapes],
        in_specs=[vmem] * len(operands),
        out_specs=[vmem] * len(out_shapes),
        cost_estimate=pl.CostEstimate(
            flops=6_000_000_000, bytes_accessed=6_000_000, transcendentals=0
        ),
        compiler_params=pltpu.CompilerParams(vmem_limit_bytes=40 * 1024 * 1024),
        name=name,
    )(*operands)


def exchange(rows, axes):
    return lax.all_to_all(rows.reshape(-1, 8, BLOCK), axes, 0, 0, tiled=True).reshape(-1, BLOCK)


def shards(query_gate, key_input, value_input, grad_output, filter_raw, skip_gain):
    tab = tables()
    key_f = key_input[0].astype(F32)
    value_f = value_input[0].astype(F32)
    out_f = grad_output[0].astype(F32)
    mixed = key_f * value_f
    gated = out_f * query_gate[0].astype(F32)
    half = filter_raw.shape[1] // 2
    taps = lax.dynamic_slice_in_dim(filter_raw, lax.axis_index("ch") * half, half, 1)
    both = ("ch", "seq")
    mixed_in = exchange(mixed.T, both)
    taps_in = exchange(taps.T.astype(F32), "seq")
    gated_in = exchange(gated.T, both)
    conv, mspec, tspec = call(
        conv_kernel,
        [(2048, BLOCK), (8, 2, 2, BLOCK, BLOCK), (8, 2, BLOCK, BLOCK)],
        (*tab, mixed_in, taps_in),
        "conv_part",
    )
    back, corr = call(
        back_kernel,
        [(2048, BLOCK), (1024, BLOCK)],
        (*tab, gated_in, mspec, tspec),
        "back_part",
    )
    conv_time = exchange(conv, both).T
    back_time = exchange(back, both).T
    grad_filter = exchange(corr, "seq").T
    conv_full = conv_time + skip_gain * mixed
    back_full = back_time + skip_gain * gated
    grad_query = (out_f * conv_full).astype(BF16)[None]
    grad_key = (back_full * value_f).astype(BF16)[None]
    grad_value = (back_full * key_f).astype(BF16)[None]
    return (grad_query, grad_key, grad_value, grad_filter)


def solution(mesh):
    in_specs = (
        P("ch", "seq", None),
        P("ch", "seq", None),
        P("ch", "seq", None),
        P("ch", "seq", None),
        P("seq", None),
        P(),
    )
    out_specs = (P("ch", "seq", None), P("ch", "seq", None), P("ch", "seq", None), P("seq", "ch"))
    return jax.shard_map(shards, mesh=mesh, in_specs=in_specs, out_specs=out_specs, check_vma=False)
```

time: 338 us -> 245 us (0.72)
  the two profiles are of different devices: /device:TPU:32 before, /device:TPU:1 now
where the time goes in v1:
time: 245 us; the launch traced here: 244 us
  waiting for transfers between devices  88.4 us (36%)
  blocking collectives  64.4 us (26%)
  starting transfers between devices  35.4 us (14%)
  local copies, waits for them, and re-layouts  27.9 us (11%)
  Pallas kernels  20.5 us (8%)
  other arithmetic  6.12 us (2%)
    all_to_all x4, waiting for transfers between devices, exchange(): lax.all_to_all(rows.reshape(-1, 8, BLOCK), axes, 0, 0, tiled=True)  88.4 us
    all_to_all x2, blocking collectives, exchange(): lax.all_to_all(rows.reshape(-1, 8, BLOCK), axes, 0, 0, tiled=True)  64.4 us
    all_to_all x4, starting transfers between devices, exchange(): lax.all_to_all(rows.reshape(-1, 8, BLOCK), axes, 0, 0, tiled=True)  35.4 us
    unnamed x83, local copies, waits for them, and re-layouts  27.9 us
    pallas_call x2, Pallas kernels, call(): pl.pallas_call(kernel, out_shape=[jax.ShapeDtypeStruct(s, F32) for s in o...  20.5 us
  transfers between devices with their start and end apart: 4, of which 4 were waited for; matrix products, arithmetic and copies ran while one was open for 2% of the time, Pallas kernels for 4%

profile of v1, /device:TPU:1, one launch (start us, length us, event | category | flops | bytes accessed | tf_op | source)
XLA Modules:
  0.0 243.7 jit_solution(12847778675870554493)
XLA Ops:
  0.7 1.0 copy-done
  2.7 16.4 %all-to-all-start.1 = ((f32[128,8,128]{2,1,0:T(8,128)}), f32[128,8,128]{2,1,0:T(8,128)S(1)}, u32[]{:S(2)}, u32[]{:S(2)}) async-start(f32[128,8,128]{2,1,0:T(8,128)} %convert_bitcast_fusion), calls=%async_computation.1 | async-start | bytes 1048576 | tf_op jit(solution)/shard_map/all_to_all | solution.py:164
  19.7 1.1 fusion.4
  20.8 18.9 %all-to-all-done.1 = f32[128,8,128]{2,1,0:T(8,128)S(1)} async-done(((f32[128,8,128]{2,1,0:T(8,128)}), f32[128,8,128]{2,1,0:T(8,128)S(1)}, u32[]{:S(2)}, u32[]{:S(2)}) %all-to-all-start.1) | async-done | bytes 524320 | tf_op jit(solution)/shard_map/all_to_all | solution.py:164
  39.8 5.3 %all-to-all-start = ((f32[256,8,128]{2,1,0:T(8,128)}), f32[256,8,128]{2,1,0:T(8,128)S(1)}, u32[]{:S(2)}, u32[]{:S(2)}) async-start(f32[256,8,128]{2,1,0:T(8,128)} %fusion.4), calls=%async_computation | async-start | bytes 2097152 | tf_op jit(solution)/shard_map/all_to_all | solution.py:164
  45.3 1.5 copy.26
  46.9 1.1 fusion.3
  48.0 28.5 %all-to-all-done = f32[256,8,128]{2,1,0:T(8,128)S(1)} async-done(((f32[256,8,128]{2,1,0:T(8,128)}), f32[256,8,128]{2,1,0:T(8,128)S(1)}, u32[]{:S(2)}, u32[]{:S(2)}) %all-to-all-start) | async-done | bytes 1048608 | tf_op jit(solution)/shard_map/all_to_all | solution.py:164
  76.4 6.1 %all-to-all-start.3 = ((f32[256,8,128]{2,1,0:T(8,128)}), f32[256,8,128]{2,1,0:T(8,128)S(1)}, u32[]{:S(2)}, u32[]{:S(2)}) async-start(f32[256,8,128]{2,1,0:T(8,128)} %fusion.3), calls=%async_computation.3 | async-start | bytes 2097152 | tf_op jit(solution)/shard_map/all_to_all | solution.py:164
  82.6 1.2 copy-done.3
  83.9 0.9 copy-done.7
  84.8 0.8 copy-done.9
  85.6 0.8 copy-done.11
  86.4 0.8 copy-done.13
  87.3 0.8 copy-done.15
  89.8 10.2 %conv_part.1 = (f32[2048,128]{1,0:T(8,128)S(1)}, f32[8,2,2,128,128]{4,3,2,1,0:T(8,128)S(1)}, f32[8,2,128,128]{3,2,1,0:T(8,128)S(1)}) custom-call(bf16[256,128]{1,0:T(8,128)(2,1)S(1)} %copy-done.15, bf16[256,128]{1,0:T(8,128)(2,1)S(1)} %copy-done.13, bf16[256,256]{1,0:T(8,128)(2,1)S(1)} %copy-done.7, bf16[256,256]{1,0:T(8,128)(2,1)S(1)} %copy-done.6, ...), custom_call_target="tpu_custom_call" | custom-call | flops 6000000000 | bytes 6000000 | tf_op jit(solution)/shard_map/conv_part/pallas_call | solution.py:150
  100.0 1.3 copy-done.21
  101.3 1.0 copy-done.23
  102.3 11.5 %all-to-all-done.3 = f32[256,8,128]{2,1,0:T(8,128)S(1)} async-done(((f32[256,8,128]{2,1,0:T(8,128)}), f32[256,8,128]{2,1,0:T(8,128)S(1)}, u32[]{:S(2)}, u32[]{:S(2)}) %all-to-all-start.3) | async-done | bytes 1048608 | tf_op jit(solution)/shard_map/all_to_all | solution.py:164
  113.8 0.9 copy-done.8
  119.8 1.6 copy-done.22
  121.4 1.2 copy-done.24
  122.6 10.3 %back_part.1 = (f32[2048,128]{1,0:T(8,128)S(1)}, f32[1024,128]{1,0:T(8,128)S(1)}) custom-call(bf16[256,128]{1,0:T(8,128)(2,1)S(1)} %copy-done.16, bf16[256,128]{1,0:T(8,128)(2,1)S(1)} %copy-done.14, bf16[256,256]{1,0:T(8,128)(2,1)S(1)} %copy-done.8, bf16[256,256]{1,0:T(8,128)(2,1)S(1)} %copy-done.6, bf16[256,256]{1,0:T(8,128)(2,1)S(1)} %copy-done.5, ...), custom_call_target="tpu_custom_call" | custom-call | flops 6000000000 | bytes 6000000 | tf_op jit(solution)/shard_map/back_part/pallas_call | solution.py:150
  133.0 27.3 %all_to_all.30 = f32[128,8,128]{2,1,0:T(8,128)S(1)} all-to-all(f32[128,8,128]{2,1,0:T(8,128)S(1)} %bitcast.75), channel_id=1, replica_groups=mesh['seq'=128,'ch'=2] {'seq'}, dimensions={0} | all-to-all | bytes 1048576 | tf_op jit(solution)/shard_map/all_to_all | solution.py:164
  160.3 37.0 %all_to_all.31 = f32[256,8,128]{2,1,0:T(8,128)} all-to-all(f32[256,8,128]{2,1,0:T(8,128)S(1)} %bitcast.71), channel_id=1, replica_groups=mesh['seq'=128,'ch'=2] {'ch','seq'}, dimensions={0} | all-to-all | bytes 2097152 | tf_op jit(solution)/shard_map/all_to_all | solution.py:164
  197.3 7.6 %all-to-all-start.4 = ((f32[256,8,128]{2,1,0:T(8,128)}), f32[256,8,128]{2,1,0:T(8,128)}, u32[]{:S(2)}, u32[]{:S(2)}) async-start(f32[256,8,128]{2,1,0:T(8,128)} %bitcast.72), calls=%async_computation.4 | async-start | bytes 2097152 | tf_op jit(solution)/shard_map/all_to_all | solution.py:164
  205.0 1.0 copy.34
  206.0 29.5 %all-to-all-done.4 = f32[256,8,128]{2,1,0:T(8,128)} async-done(((f32[256,8,128]{2,1,0:T(8,128)}), f32[256,8,128]{2,1,0:T(8,128)}, u32[]{:S(2)}, u32[]{:S(2)}) %all-to-all-start.4) | async-done | bytes 1048608 | tf_op jit(solution)/shard_map/all_to_all | solution.py:164
  235.5 3.1 %fusion.5 = (bf16[1,128,2048]{1,2,0:T(8,128)(2,1)}, bf16[1,128,2048]{1,2,0:T(8,128)(2,1)}, bf16[1,128,2048]{1,2,0:T(8,128)(2,1)S(1)}) fusion(bf16[1,128,2048]{1,2,0:T(8,128)(2,1)S(1)} %copy-done.26, bf16[1,128,2048]{1,2,0:T(8,128)(2,1)S(1)} %copy-done.30, bf16[1,128,2048]{1,2,0:T(8,128)(2,1)S(1)} %copy-done.32, f32[2048]{0:T(1024)S(1)} %copy-done.36, ...), kind=kLoop, calls=%fused_computation.12 | loop fusion | flops 4194304 | bytes 5775360 | tf_op jit(solution)/shard_map/broadcast_in_dim | solution.py:199
  238.6 2.0 copy.33
  240.7 2.0 copy.32
  242.7 1.0 copy.31
  (68 shorter events, 8.7 us)
Async XLA Ops:
  0.6 1.0 copy-start
  0.6 18.5 %copy-start.33 = (bf16[1,128,2048]{2,1,0:T(8,128)(2,1)S(1)}, bf16[1,128,2048]{2,1,0:T(8,128)(2,1)}, u32[]{:S(2)}) copy-start(bf16[1,128,2048]{2,1,0:T(8,128)(2,1)} %param.17) | copy-start | bytes 1572868
  0.7 18.7 %copy-start.34 = (bf16[1,128,2048]{2,1,0:T(8,128)(2,1)S(1)}, bf16[1,128,2048]{2,1,0:T(8,128)(2,1)}, u32[]{:S(2)}) copy-start(bf16[1,128,2048]{2,1,0:T(8,128)(2,1)} %param.18) | copy-start | bytes 1572868
  2.7 37.1 %all-to-all-start.1 = ((f32[128,8,128]{2,1,0:T(8,128)}), f32[128,8,128]{2,1,0:T(8,128)S(1)}, u32[]{:S(2)}, u32[]{:S(2)}) async-start(f32[128,8,128]{2,1,0:T(8,128)} %convert_bitcast_fusion), calls=%async_computation.1 | async-start | bytes 1048576 | tf_op jit(solution)/shard_map/all_to_all | solution.py:164
  19.4 20.4 %copy-start.25 = (bf16[1,128,2048]{1,2,0:T(8,128)(2,1)}, bf16[1,128,2048]{1,2,0:T(8,128)(2,1)S(1)}, u32[]{:S(2)}) copy-start(bf16[1,128,2048]{1,2,0:T(8,128)(2,1)S(1)} %copy.27) | copy-start | bytes 1572868
  19.7 20.1 %copy-start.27 = (bf16[1,128,2048]{1,2,0:T(8,128)(2,1)}, bf16[1,128,2048]{1,2,0:T(8,128)(2,1)S(1)}, u32[]{:S(2)}) copy-start(bf16[1,128,2048]{1,2,0:T(8,128)(2,1)S(1)} %copy.28) | copy-start | bytes 1572868
  19.7 25.3 %copy-start.35 = (bf16[1,128,2048]{2,1,0:T(8,128)(2,1)S(1)}, bf16[1,128,2048]{2,1,0:T(8,128)(2,1)}, u32[]{:S(2)}) copy-start(bf16[1,128,2048]{2,1,0:T(8,128)(2,1)} %param.16) | copy-start | bytes 1572868
  39.8 36.7 %all-to-all-start = ((f32[256,8,128]{2,1,0:T(8,128)}), f32[256,8,128]{2,1,0:T(8,128)S(1)}, u32[]{:S(2)}, u32[]{:S(2)}) async-start(f32[256,8,128]{2,1,0:T(8,128)} %fusion.4), calls=%async_computation | async-start | bytes 2097152 | tf_op jit(solution)/shard_map/all_to_all | solution.py:164
  45.3 31.1 %copy-start.29 = (bf16[1,128,2048]{1,2,0:T(8,128)(2,1)}, bf16[1,128,2048]{1,2,0:T(8,128)(2,1)S(1)}, u32[]{:S(2)}) copy-start(bf16[1,128,2048]{1,2,0:T(8,128)(2,1)S(1)} %copy.30) | copy-start | bytes 1572868
  46.8 29.6 %copy-start.31 = (bf16[1,128,2048]{1,2,0:T(8,128)(2,1)}, bf16[1,128,2048]{1,2,0:T(8,128)(2,1)S(1)}, u32[]{:S(2)}) copy-start(bf16[1,128,2048]{1,2,0:T(8,128)(2,1)S(1)} %copy.26) | copy-start | bytes 1572868
  46.9 35.7 %copy-start.4 = (bf16[256,256]{1,0:T(8,128)(2,1)S(1)}, bf16[256,256]{1,0:T(8,128)(2,1)}, u32[]{:S(2)}) copy-start(bf16[256,256]{1,0:T(8,128)(2,1)} %constant.43.refs_5_) | copy-start | bytes 393220
  46.9 35.7 %copy-start.5 = (bf16[256,256]{1,0:T(8,128)(2,1)S(1)}, bf16[256,256]{1,0:T(8,128)(2,1)}, u32[]{:S(2)}) copy-start(bf16[256,256]{1,0:T(8,128)(2,1)} %constant.40.refs_4_) | copy-start | bytes 393220
  46.9 35.7 %copy-start.6 = (bf16[256,256]{1,0:T(8,128)(2,1)S(1)}, bf16[256,256]{1,0:T(8,128)(2,1)}, u32[]{:S(2)}) copy-start(bf16[256,256]{1,0:T(8,128)(2,1)} %constant.39.refs_3_) | copy-start | bytes 393220
  76.4 6.2 %copy-start.2 = (f32[256,8,128]{2,1,0:T(8,128)}, f32[256,8,128]{2,1,0:T(8,128)S(1)}, u32[]{:S(2)}) copy-start(f32[256,8,128]{2,1,0:T(8,128)S(1)} %all-to-all-done) | copy-start | bytes 3145732
  76.4 37.4 %all-to-all-start.3 = ((f32[256,8,128]{2,1,0:T(8,128)}), f32[256,8,128]{2,1,0:T(8,128)S(1)}, u32[]{:S(2)}, u32[]{:S(2)}) async-start(f32[256,8,128]{2,1,0:T(8,128)} %fusion.3), calls=%async_computation.3 | async-start | bytes 2097152 | tf_op jit(solution)/shard_map/all_to_all | solution.py:164
  82.6 1.2 copy-start.3
  83.9 0.9 copy-start.7
  84.8 0.8 copy-start.9
  85.6 0.8 copy-start.11
  86.4 0.8 copy-start.13
  100.0 1.3 copy-start.21
  101.3 1.0 copy-start.23
  113.8 0.9 copy-start.8
  119.8 1.6 copy-start.22
  121.4 1.2 copy-start.24
  132.9 64.4 %copy-start.1 = (f32[2048,128]{1,0:T(8,128)}, f32[2048,128]{1,0:T(8,128)S(1)}, u32[]{:S(2)}) copy-start(f32[2048,128]{1,0:T(8,128)S(1)} %get-tuple-element.12) | copy-start | bytes 3145732
  197.3 38.2 %copy-start.26 = (bf16[1,128,2048]{1,2,0:T(8,128)(2,1)S(1)}, bf16[1,128,2048]{1,2,0:T(8,128)(2,1)}, u32[]{:S(2)}) copy-start(bf16[1,128,2048]{1,2,0:T(8,128)(2,1)} %copy-done.25) | copy-start | bytes 1572868
  197.3 38.2 %copy-start.28 = (bf16[1,128,2048]{1,2,0:T(8,128)(2,1)S(1)}, bf16[1,128,2048]{1,2,0:T(8,128)(2,1)}, u32[]{:S(2)}) copy-start(bf16[1,128,2048]{1,2,0:T(8,128)(2,1)} %copy-done.27) | copy-start | bytes 1572868
  197.3 38.2 %copy-start.30 = (bf16[1,128,2048]{1,2,0:T(8,128)(2,1)S(1)}, bf16[1,128,2048]{1,2,0:T(8,128)(2,1)}, u32[]{:S(2)}) copy-start(bf16[1,128,2048]{1,2,0:T(8,128)(2,1)} %copy-done.29) | copy-start | bytes 1572868
  197.3 38.2 %copy-start.32 = (bf16[1,128,2048]{1,2,0:T(8,128)(2,1)S(1)}, bf16[1,128,2048]{1,2,0:T(8,128)(2,1)}, u32[]{:S(2)}) copy-start(bf16[1,128,2048]{1,2,0:T(8,128)(2,1)} %copy-done.31) | copy-start | bytes 1572868
  197.3 38.2 %copy-start.36 = (f32[2048]{0:T(1024)S(1)}, f32[2048]{0:T(1024)}, u32[]{:S(2)}) copy-start(f32[2048]{0:T(1024)} %param.21) | copy-start | bytes 24580
  197.3 38.2 %all-to-all-start.4 = ((f32[256,8,128]{2,1,0:T(8,128)}), f32[256,8,128]{2,1,0:T(8,128)}, u32[]{:S(2)}, u32[]{:S(2)}) async-start(f32[256,8,128]{2,1,0:T(8,128)} %bitcast.72), calls=%async_computation.4 | async-start | bytes 2097152 | tf_op jit(solution)/shard_map/all_to_all | solution.py:164
  (9 other events, 7.6 us)

commit v2 on v1

v2 whole, which is shorter than its diff:
```python
import math

import jax
import jax.numpy as jnp
import numpy as np
from jax import lax
from jax.experimental import pallas as pl
from jax.experimental.pallas import tpu as pltpu
from jax.sharding import PartitionSpec as P

BLOCK = 128
FULL = 2 * BLOCK * BLOCK
F32 = jnp.float32
BF16 = jnp.bfloat16


def split_table(table):
    high = jnp.asarray(table, F32).astype(BF16)
    low = (jnp.asarray(table, F32) - high.astype(F32)).astype(BF16)
    return (high, low)


def tables():
    idx = np.arange(BLOCK)
    turn_one = 2.0 * math.pi / (2 * BLOCK) * ((idx[:, None] + 0.5) * idx[None, :])
    first = np.concatenate([np.cos(turn_one), -np.sin(turn_one)], axis=0)
    turn_two = 2.0 * math.pi / BLOCK * (idx[:, None] * idx[None, :] % BLOCK)
    cos_two, sin_two = np.cos(turn_two), np.sin(turn_two)
    second = np.block([[cos_two, -sin_two], [sin_two, cos_two]])
    second_inv = np.block([[cos_two, sin_two], [-sin_two, cos_two]])
    turn_mid = 2.0 * math.pi / FULL * ((idx[:, None] + 0.5) * idx[None, :])
    f_high, f_low = split_table(first.astype(np.float32))
    rows = [jnp.concatenate([f_high, f_low], axis=1)]
    for table in (second, second_inv, first.T):
        rows.extend(split_table(table.astype(np.float32)))
    mid = np.concatenate([np.cos(turn_mid), np.sin(turn_mid)], axis=0)
    return (jnp.concatenate(rows, axis=0), jnp.asarray(mid, F32))


def halves(x):
    high = x.astype(BF16)
    return (high, (x - high.astype(F32)).astype(BF16))


def dot(a, b):
    return jnp.dot(a, b, preferred_element_type=F32)


def dot_left(high, low, x):
    x_high, x_low = halves(x)
    return dot(high, x_high) + dot(low, x_high) + dot(high, x_low)


def dot_right(x, high, low):
    x_high, x_low = halves(x)
    return dot(x_high, high) + dot(x_high, low) + dot(x_low, high)


def to_spectrum(parts, tab, mid):
    cos_mid, sin_mid = mid[:BLOCK], mid[BLOCK:]
    lines = dot_left(tab[:256, :BLOCK], tab[:256, BLOCK:], jnp.concatenate(parts, axis=1))
    rows = []
    for i in range(len(parts)):
        re = lines[:BLOCK, i * BLOCK : (i + 1) * BLOCK]
        im = lines[BLOCK:, i * BLOCK : (i + 1) * BLOCK]
        rows.append(
            jnp.concatenate([re * cos_mid + im * sin_mid, im * cos_mid - re * sin_mid], axis=1)
        )
    spec = dot_right(jnp.concatenate(rows, axis=0), tab[256:512], tab[512:768])
    return [
        (spec[i * BLOCK : (i + 1) * BLOCK, :BLOCK], spec[i * BLOCK : (i + 1) * BLOCK, BLOCK:])
        for i in range(len(parts))
    ]


def from_spectrum(specs, tab, mid):
    cos_mid, sin_mid = mid[:BLOCK], mid[BLOCK:]
    rows = jnp.concatenate([jnp.concatenate([re, im], axis=1) for re, im in specs], axis=0)
    grid = dot_right(rows, tab[768:1024], tab[1024:1280])
    cols = []
    for i in range(len(specs)):
        re = grid[i * BLOCK : (i + 1) * BLOCK, :BLOCK]
        im = grid[i * BLOCK : (i + 1) * BLOCK, BLOCK:]
        cols.append(
            jnp.concatenate([re * cos_mid - im * sin_mid, im * cos_mid + re * sin_mid], axis=0)
        )
    lines = dot_left(tab[1280:1408], tab[1408:1536], jnp.concatenate(cols, axis=1))
    return [lines[:, i * BLOCK : (i + 1) * BLOCK] for i in range(len(specs))]


SCALE = 1.0 / (BLOCK * (FULL // 2))
OWNED = 8
WIDTH = 2048
HALF = WIDTH // 2
MESH = pl.DeviceIdType.MESH


def channel_rows(part, channel):
    return pl.ds(part * BLOCK * OWNED + channel, BLOCK, stride=OWNED)


def tile(index):
    return pl.ds(pl.multiple_of(index * OWNED, OWNED), OWNED)


def peer(step, seq, ch):
    turn = step % 8
    near = (turn + 1) // 2
    shift = (turn % 2) * near + (1 - turn % 2) * (8 - near)
    z = (seq // 16 + shift) % 8
    rest = ((seq % 16) * 2 + ch + step // 8) % 32
    return (z * 16 + rest // 2, rest % 2)


def peer_same(step, seq):
    turn = step % 8
    near = (turn + 1) // 2
    shift = (turn % 2) * near + (1 - turn % 2) * (8 - near)
    z = (seq // 16 + shift) % 8
    return z * 16 + (seq % 16 + step // 8) % 16


def send_all(source, target, send, recv):
    seq, ch = lax.axis_index("seq"), lax.axis_index("ch")
    me = ch * BLOCK + seq

    def body(step, carry):
        to_seq, to_ch = peer(step, seq, ch)
        pltpu.make_async_remote_copy(
            src_ref=source.at[tile(to_ch * BLOCK + to_seq)],
            dst_ref=target.at[tile(me)],
            send_sem=send,
            recv_sem=recv,
            device_id=(to_seq, to_ch),
            device_id_type=MESH,
        ).start()
        return carry

    lax.fori_loop(1, 2 * BLOCK, body, 0)
    target[tile(me), :] = source[tile(me), :]


def send_same(source, target, send, recv):
    seq, ch = lax.axis_index("seq"), lax.axis_index("ch")

    def body(step, carry):
        to_seq = peer_same(step, seq)
        pltpu.make_async_remote_copy(
            src_ref=source.at[tile(to_seq)],
            dst_ref=target.at[tile(seq)],
            send_sem=send,
            recv_sem=recv,
            device_id=(to_seq, ch),
            device_id_type=MESH,
        ).start()
        return carry

    lax.fori_loop(1, BLOCK, body, 0)
    target[tile(seq), :] = source[tile(seq), :]


def wait_rows(ref, rows, sem):
    part = ref.at[pl.ds(0, rows)]
    pltpu.make_async_copy(part, part, sem).wait()


ALL_ROWS = WIDTH - OWNED
SAME_ROWS = HALF - OWNED


def kernel(
    query_hbm,
    key_hbm,
    value_hbm,
    out_hbm,
    filter_hbm,
    gain_ref,
    tab_hbm,
    mid_hbm,
    grad_query,
    grad_key,
    grad_value,
    grad_filter,
    query,
    key,
    value,
    out,
    taps,
    tab_ref,
    mid_ref,
    mixed_t,
    gated_t,
    taps_t,
    mixed_in,
    gated_in,
    taps_in,
    conv,
    back,
    corr,
    conv_in,
    back_in,
    corr_in,
    mspec,
    tspec,
    load,
    send,
    recv,
):
    seq, ch = lax.axis_index("seq"), lax.axis_index("ch")
    barrier = pltpu.get_barrier_semaphore()

    loads = [
        pltpu.make_async_copy(key_hbm.at[0], key, load.at[0]),
        pltpu.make_async_copy(value_hbm.at[0], value, load.at[1]),
        pltpu.make_async_copy(
            filter_hbm.at[:, pl.ds(pl.multiple_of(ch * HALF, HALF), HALF)], taps, load.at[2]
        ),
        pltpu.make_async_copy(out_hbm.at[0], out, load.at[3]),
        pltpu.make_async_copy(query_hbm.at[0], query, load.at[4]),
        pltpu.make_async_copy(tab_hbm, tab_ref, load.at[5]),
        pltpu.make_async_copy(mid_hbm, mid_ref, load.at[6]),
    ]
    for copy in loads:
        copy.start()

    def greet(step, carry):
        to_seq, to_ch = peer(step, seq, ch)
        pl.semaphore_signal(barrier, inc=1, device_id=(to_seq, to_ch), device_id_type=MESH)
        return carry

    lax.fori_loop(1, 2 * BLOCK, greet, 0)

    def flip_product(left, right, target):
        def body(j, carry):
            cols = pl.ds(pl.multiple_of(j * BLOCK, BLOCK), BLOCK)
            target[cols, :] = (left[:, cols].astype(F32) * right[:, cols].astype(F32)).T
            return carry

        lax.fori_loop(0, WIDTH // BLOCK, body, 0)

    loads[0].wait()
    loads[1].wait()
    flip_product(key, value, mixed_t)
    loads[2].wait()

    def flip_taps(j, carry):
        cols = pl.ds(pl.multiple_of(j * BLOCK, BLOCK), BLOCK)
        taps_t[cols, :] = taps[:, cols].astype(F32).T
        return carry

    lax.fori_loop(0, HALF // BLOCK, flip_taps, 0)
    pl.semaphore_wait(barrier, 2 * BLOCK - 1)
    send_all(mixed_t, mixed_in, send.at[0], recv.at[0])
    send_same(taps_t, taps_in, send.at[1], recv.at[1])
    loads[3].wait()
    loads[4].wait()
    flip_product(out, query, gated_t)
    send_all(gated_t, gated_in, send.at[2], recv.at[2])
    loads[5].wait()
    loads[6].wait()
    wait_rows(mixed_in, ALL_ROWS, recv.at[0])
    wait_rows(taps_in, SAME_ROWS, recv.at[1])

    def conv_body(c, carry):
        tab, mid = tab_ref[...], mid_ref[...]
        parts = [mixed_in[channel_rows(b, c), :] for b in range(2)]
        parts.append(taps_in[channel_rows(0, c), :])
        mixed_a, mixed_b, taps_spec = to_spectrum(parts, tab, mid)
        t_re, t_im = taps_spec
        prods = []
        for b, (re, im) in enumerate((mixed_a, mixed_b)):
            mspec[c, b, 0] = re
            mspec[c, b, 1] = im
            prods.append((re * t_re - im * t_im, re * t_im + im * t_re))
        tspec[c, 0] = t_re
        tspec[c, 1] = t_im
        lines = from_spectrum(prods, tab, mid)
        for b in range(2):
            conv[channel_rows(b, c), :] = lines[b] * SCALE
        return carry

    lax.fori_loop(0, OWNED, conv_body, 0)
    send_all(conv, conv_in, send.at[3], recv.at[3])
    wait_rows(gated_in, ALL_ROWS, recv.at[2])

    def back_body(c, carry):
        tab, mid = tab_ref[...], mid_ref[...]
        gated = to_spectrum([gated_in[channel_rows(b, c), :] for b in range(2)], tab, mid)
        t_re, t_im = tspec[c, 0], tspec[c, 1]
        prods = []
        terms = []
        for b, (re, im) in enumerate(gated):
            m_re, m_im = mspec[c, b, 0], mspec[c, b, 1]
            prods.append((t_re * re + t_im * im, t_re * im - t_im * re))
            terms.append((m_re * re + m_im * im, m_re * im - m_im * re))
        prods.append((terms[0][0] + terms[1][0], terms[0][1] + terms[1][1]))
        lines = from_spectrum(prods, tab, mid)
        for b in range(2):
            back[channel_rows(b, c), :] = lines[b] * SCALE
        corr[channel_rows(0, c), :] = lines[2] * SCALE
        return carry

    lax.fori_loop(0, OWNED, back_body, 0)
    send_all(back, back_in, send.at[4], recv.at[4])
    send_same(corr, corr_in, send.at[5], recv.at[5])

    wait_rows(conv_in, ALL_ROWS, recv.at[3])

    def query_body(j, carry):
        cols = pl.ds(pl.multiple_of(j * BLOCK, BLOCK), BLOCK)
        mixed = key[:, cols].astype(F32) * value[:, cols].astype(F32)
        full = conv_in[cols, :].T + gain_ref[:, cols] * mixed
        grad_query[0, :, cols] = (out[:, cols].astype(F32) * full).astype(BF16)
        return carry

    lax.fori_loop(0, WIDTH // BLOCK, query_body, 0)
    wait_rows(back_in, ALL_ROWS, recv.at[4])

    def back_out(j, carry):
        cols = pl.ds(pl.multiple_of(j * BLOCK, BLOCK), BLOCK)
        gated = out[:, cols].astype(F32) * query[:, cols].astype(F32)
        full = back_in[cols, :].T + gain_ref[:, cols] * gated
        grad_key[0, :, cols] = (full * value[:, cols].astype(F32)).astype(BF16)
        grad_value[0, :, cols] = (full * key[:, cols].astype(F32)).astype(BF16)
        return carry

    lax.fori_loop(0, WIDTH // BLOCK, back_out, 0)
    wait_rows(corr_in, SAME_ROWS, recv.at[5])

    def filter_out(j, carry):
        cols = pl.ds(pl.multiple_of(j * BLOCK, BLOCK), BLOCK)
        grad_filter[:, cols] = corr_in[cols, :].T
        return carry

    lax.fori_loop(0, HALF // BLOCK, filter_out, 0)
    wait_rows(mixed_t, ALL_ROWS, send.at[0])
    wait_rows(taps_t, SAME_ROWS, send.at[1])
    wait_rows(gated_t, ALL_ROWS, send.at[2])
    wait_rows(conv, ALL_ROWS, send.at[3])
    wait_rows(back, ALL_ROWS, send.at[4])
    wait_rows(corr, SAME_ROWS, send.at[5])


def shards(query_gate, key_input, value_input, grad_output, filter_raw, skip_gain):
    tab, mid = tables()
    anywhere = pl.BlockSpec(memory_space=pl.ANY)
    vmem = pl.BlockSpec(memory_space=pltpu.VMEM)
    signal = jax.ShapeDtypeStruct((1, BLOCK, WIDTH), BF16)
    narrow = pltpu.VMEM((BLOCK, WIDTH), BF16)
    tall = pltpu.VMEM((WIDTH, BLOCK), F32)
    short = pltpu.VMEM((HALF, BLOCK), F32)
    return tuple(
        pl.pallas_call(
            kernel,
            out_shape=[signal, signal, signal, jax.ShapeDtypeStruct((BLOCK, HALF), F32)],
            in_specs=[anywhere] * 5 + [vmem] + [anywhere] * 2,
            out_specs=[vmem] * 4,
            scratch_shapes=[narrow] * 4
            + [
                pltpu.VMEM((BLOCK, HALF), BF16),
                pltpu.VMEM(tab.shape, BF16),
                pltpu.VMEM(mid.shape, F32),
            ]
            + [tall, tall, short] * 4
            + [
                pltpu.VMEM((OWNED, 2, 2, BLOCK, BLOCK), F32),
                pltpu.VMEM((OWNED, 2, BLOCK, BLOCK), F32),
                pltpu.SemaphoreType.DMA((7,)),
                pltpu.SemaphoreType.DMA((6,)),
                pltpu.SemaphoreType.DMA((6,)),
            ],
            compiler_params=pltpu.CompilerParams(
                collective_id=0, has_side_effects=True, vmem_limit_bytes=60 * 1024 * 1024
            ),
            name="hyena_back",
        )(
            query_gate,
            key_input,
            value_input,
            grad_output,
            filter_raw,
            skip_gain.reshape(1, WIDTH),
            tab,
            mid,
        )
    )


def solution(mesh):
    in_specs = (
        P("ch", "seq", None),
        P("ch", "seq", None),
        P("ch", "seq", None),
        P("ch", "seq", None),
        P("seq", None),
        P(),
    )
    out_specs = (P("ch", "seq", None), P("ch", "seq", None), P("ch", "seq", None), P("seq", "ch"))
    return jax.shard_map(shards, mesh=mesh, in_specs=in_specs, out_specs=out_specs, check_vma=False)
```

time: 245 us -> 146 us (0.60)
  Pallas kernels: 20.5 us -> 140 us
  waiting for transfers between devices: 88.4 us -> 0 us
  blocking collectives: 64.4 us -> 0 us
  starting transfers between devices: 35.4 us -> 0 us
  local copies, waits for them, and re-layouts: 27.9 us -> 5.19 us
  other arithmetic: 6.12 us -> 0 us
    pallas_call x2 -> x1, Pallas kernels: 20.5 us -> 140 us  [shards(): pl.pallas_call(kernel, out_shape=[signal, signal, signal, jax.ShapeDtypeS...]
    all_to_all x4 -> x0, waiting for transfers between devices: 88.4 us -> none  [exchange(): lax.all_to_all(rows.reshape(-1, 8, BLOCK), axes, 0, 0, tiled=True)]
    all_to_all x2 -> x0, blocking collectives: 64.4 us -> none  [exchange(): lax.all_to_all(rows.reshape(-1, 8, BLOCK), axes, 0, 0, tiled=True)]
    all_to_all x4 -> x0, starting transfers between devices: 35.4 us -> none  [exchange(): lax.all_to_all(rows.reshape(-1, 8, BLOCK), axes, 0, 0, tiled=True)]
    unnamed x83 -> x10, local copies, waits for them, and re-layouts: 27.9 us -> 5.19 us
    broadcast_in_dim x1 -> x0, other arithmetic: 3.1 us -> none  [shards(): grad_value = (back_full * key_f).astype(BF16)[None]]
    reshape x3 -> x0, other arithmetic: 3.02 us -> none  [exchange(): rows.reshape(-1, 8, BLOCK)]
  transfers between devices with their start and end apart: 4 -> 0, of which waited for: 4 -> 0; matrix products, arithmetic and copies ran while one was open for 2% -> 0% of each run, Pallas kernels for 4% -> 0%
where the time goes in v2:
time: 146 us
  Pallas kernels  140 us (96%)
  local copies, waits for them, and re-layouts  5.19 us (4%)
    pallas_call x1, Pallas kernels, shards(): pl.pallas_call(kernel, out_shape=[signal, signal, signal, jax.ShapeDtypeS...  140 us
    unnamed x10, local copies, waits for them, and re-layouts  5.19 us

profile of v2, /device:TPU:1, one launch (start us, length us, event | category | flops | bytes accessed | tf_op | source)
XLA Modules:
  0.0 145.7 jit_solution(4102154948332948235)
XLA Ops:
  0.6 139.8 %hyena_back.1 = (bf16[1,128,2048]{2,1,0:T(8,128)(2,1)}, bf16[1,128,2048]{2,1,0:T(8,128)(2,1)}, bf16[1,128,2048]{2,1,0:T(8,128)(2,1)}, f32[128,1024]{1,0:T(8,128)}) custom-call(bf16[1,128,2048]{2,1,0:T(8,128)(2,1)} %query_hbm.1, bf16[1,128,2048]{2,1,0:T(8,128)(2,1)} %key_hbm.1, bf16[1,128,2048]{2,1,0:T(8,128)(2,1)} %value_hbm.1, ...), custom_call_target="tpu_custom_call" | custom-call | tf_op jit(solution)/shard_map/hyena_back/pallas_call | solution.py:353
  140.5 0.0 copy-start.2
  140.5 1.9 %copy.23 = bf16[1,128,2048]{2,1,0:T(8,128)(2,1)} copy(bf16[1,128,2048]{2,1,0:T(8,128)(2,1)} %get-tuple-element.8) | data formatting | bytes 1048576
  142.4 0.0 copy-done.2
  142.4 0.0 copy-start.1
  142.4 0.8 copy.24
  143.2 0.4 copy-done.1
  143.7 0.0 copy-start
  143.7 0.8 copy.25
  144.5 0.4 copy-done
  144.9 0.8 copy.26
Async XLA Ops:
  140.5 2.0 %copy-start.2 = (bf16[1,128,2048]{2,1,0:T(8,128)(2,1)S(1)}, bf16[1,128,2048]{2,1,0:T(8,128)(2,1)}, u32[]{:S(2)}) copy-start(bf16[1,128,2048]{2,1,0:T(8,128)(2,1)} %get-tuple-element.9) | copy-start | bytes 1572868
  142.4 1.2 copy-start.1
  143.7 1.2 copy-start

commit v3 on v2

--- a/solution.py
+++ b/solution.py
@@ -103,29 +103,54 @@
     return pl.ds(pl.multiple_of(index * OWNED, OWNED), OWNED)
 
 
-def peer(step, seq, ch):
-    turn = step % 8
-    near = (turn + 1) // 2
-    shift = (turn % 2) * near + (1 - turn % 2) * (8 - near)
-    z = (seq // 16 + shift) % 8
-    rest = ((seq % 16) * 2 + ch + step // 8) % 32
-    return (z * 16 + rest // 2, rest % 2)
-
-
-def peer_same(step, seq):
-    turn = step % 8
-    near = (turn + 1) // 2
-    shift = (turn % 2) * near + (1 - turn % 2) * (8 - near)
-    z = (seq // 16 + shift) % 8
-    return z * 16 + (seq % 16 + step // 8) % 16
+TURNS = (0, 1, 7, 2, 6, 3, 5, 4)
+SLAB = BLOCK // 8
+FAR_FIRST = ((4, 0), (3, 5), (2, 6), (1, 7))
+
+
+def for_each_peer(visit, turns=TURNS):
+    seq, ch = lax.axis_index("seq"), lax.axis_index("ch")
+    z = lax.div(seq, SLAB)
+    place = lax.rem(seq, SLAB) * 2 + ch
+    bases = [lax.rem(z + turn, 8) * SLAB for turn in turns]
+
+    def at(rest, chosen):
+        low, to_ch = lax.div(rest, 2), lax.rem(rest, 2)
+        for base in chosen:
+            visit(base + low, to_ch)
+
+    def body(step, carry):
+        at(lax.rem(place + step, 2 * SLAB), bases)
+        return carry
+
+    at(place, [base for base, turn in zip(bases, turns) if turn])
+    lax.fori_loop(1, 2 * SLAB, body, 0)
+
+
+def for_each_same(visit, groups=(TURNS,)):
+    seq = lax.axis_index("seq")
+    z = lax.div(seq, SLAB)
+    place = lax.rem(seq, SLAB)
+    for turns in groups:
+        bases = [lax.rem(z + turn, 8) * SLAB for turn in turns]
+
+        def body(step, carry, bases=bases):
+            low = lax.rem(place + step, SLAB)
+            for base in bases:
+                visit(base + low)
+            return carry
+
+        for base, turn in zip(bases, turns):
+            if turn:
+                visit(base + place)
+        lax.fori_loop(1, SLAB, body, 0)
 
 
 def send_all(source, target, send, recv):
     seq, ch = lax.axis_index("seq"), lax.axis_index("ch")
     me = ch * BLOCK + seq
 
-    def body(step, carry):
-        to_seq, to_ch = peer(step, seq, ch)
+    def visit(to_seq, to_ch):
         pltpu.make_async_remote_copy(
             src_ref=source.at[tile(to_ch * BLOCK + to_seq)],
             dst_ref=target.at[tile(me)],
@@ -134,17 +159,15 @@
             device_id=(to_seq, to_ch),
             device_id_type=MESH,
         ).start()
-        return carry
-
-    lax.fori_loop(1, 2 * BLOCK, body, 0)
+
+    for_each_peer(visit)
     target[tile(me), :] = source[tile(me), :]
 
 
-def send_same(source, target, send, recv):
+def send_same(source, target, send, recv, groups=(TURNS,)):
     seq, ch = lax.axis_index("seq"), lax.axis_index("ch")
 
-    def body(step, carry):
-        to_seq = peer_same(step, seq)
+    def visit(to_seq):
         pltpu.make_async_remote_copy(
             src_ref=source.at[tile(to_seq)],
             dst_ref=target.at[tile(seq)],
@@ -153,9 +176,8 @@
             device_id=(to_seq, ch),
             device_id_type=MESH,
         ).start()
-        return carry
-
-    lax.fori_loop(1, BLOCK, body, 0)
+
+    for_each_same(visit, groups)
     target[tile(seq), :] = source[tile(seq), :]
 
 
@@ -174,13 +196,13 @@
     value_hbm,
     out_hbm,
     filter_hbm,
-    gain_ref,
+    gain_hbm,
     tab_hbm,
     mid_hbm,
     grad_query,
     grad_key,
     grad_value,
-    grad_filter,
+    corr_in,
     query,
     key,
     value,
@@ -188,6 +210,7 @@
     taps,
     tab_ref,
     mid_ref,
+    gain_ref,
     mixed_t,
     gated_t,
     taps_t,
@@ -199,7 +222,6 @@
     corr,
     conv_in,
     back_in,
-    corr_in,
     mspec,
     tspec,
     load,
@@ -219,16 +241,16 @@
         pltpu.make_async_copy(query_hbm.at[0], query, load.at[4]),
         pltpu.make_async_copy(tab_hbm, tab_ref, load.at[5]),
         pltpu.make_async_copy(mid_hbm, mid_ref, load.at[6]),
+        pltpu.make_async_copy(gain_hbm, gain_ref, load.at[7]),
     ]
     for copy in loads:
         copy.start()
 
-    def greet(step, carry):
-        to_seq, to_ch = peer(step, seq, ch)
+    def greet(to_seq, to_ch):
         pl.semaphore_signal(barrier, inc=1, device_id=(to_seq, to_ch), device_id_type=MESH)
-        return carry
-
-    lax.fori_loop(1, 2 * BLOCK, greet, 0)
+
+    with jax.named_scope("greet"):
+        for_each_peer(greet, TURNS[::-1])
 
     def flip_product(left, right, target):
         def body(j, carry):
@@ -238,9 +260,11 @@
 
         lax.fori_loop(0, WIDTH // BLOCK, body, 0)
 
-    loads[0].wait()
-    loads[1].wait()
-    flip_product(key, value, mixed_t)
+    with jax.named_scope("load"):
+        loads[0].wait()
+        loads[1].wait()
+    with jax.named_scope("flip_mixed"):
+        flip_product(key, value, mixed_t)
     loads[2].wait()
 
     def flip_taps(j, carry):
@@ -248,18 +272,26 @@
         taps_t[cols, :] = taps[:, cols].astype(F32).T
         return carry
 
-    lax.fori_loop(0, HALF // BLOCK, flip_taps, 0)
-    pl.semaphore_wait(barrier, 2 * BLOCK - 1)
-    send_all(mixed_t, mixed_in, send.at[0], recv.at[0])
-    send_same(taps_t, taps_in, send.at[1], recv.at[1])
+    with jax.named_scope("flip_taps"):
+        lax.fori_loop(0, HALF // BLOCK, flip_taps, 0)
+    with jax.named_scope("barrier"):
+        pl.semaphore_wait(barrier, 2 * BLOCK - 1)
+    with jax.named_scope("send_mixed"):
+        send_all(mixed_t, mixed_in, send.at[0], recv.at[0])
+    with jax.named_scope("send_taps"):
+        send_same(taps_t, taps_in, send.at[1], recv.at[1])
     loads[3].wait()
     loads[4].wait()
-    flip_product(out, query, gated_t)
-    send_all(gated_t, gated_in, send.at[2], recv.at[2])
+    with jax.named_scope("flip_gated"):
+        flip_product(out, query, gated_t)
+    with jax.named_scope("send_gated"):
+        send_all(gated_t, gated_in, send.at[2], recv.at[2])
     loads[5].wait()
     loads[6].wait()
-    wait_rows(mixed_in, ALL_ROWS, recv.at[0])
-    wait_rows(taps_in, SAME_ROWS, recv.at[1])
+    loads[7].wait()
+    with jax.named_scope("wait_mixed"):
+        wait_rows(mixed_in, ALL_ROWS, recv.at[0])
+        wait_rows(taps_in, SAME_ROWS, recv.at[1])
 
     def conv_body(c, carry):
         tab, mid = tab_ref[...], mid_ref[...]
@@ -279,9 +311,12 @@
             conv[channel_rows(b, c), :] = lines[b] * SCALE
         return carry
 
-    lax.fori_loop(0, OWNED, conv_body, 0)
-    send_all(conv, conv_in, send.at[3], recv.at[3])
-    wait_rows(gated_in, ALL_ROWS, recv.at[2])
+    with jax.named_scope("conv"):
+        lax.fori_loop(0, OWNED, conv_body, 0)
+    with jax.named_scope("send_conv"):
+        send_all(conv, conv_in, send.at[3], recv.at[3])
+    with jax.named_scope("wait_gated"):
+        wait_rows(gated_in, ALL_ROWS, recv.at[2])
 
     def back_body(c, carry):
         tab, mid = tab_ref[...], mid_ref[...]
@@ -300,11 +335,14 @@
         corr[channel_rows(0, c), :] = lines[2] * SCALE
         return carry
 
-    lax.fori_loop(0, OWNED, back_body, 0)
-    send_all(back, back_in, send.at[4], recv.at[4])
-    send_same(corr, corr_in, send.at[5], recv.at[5])
-
-    wait_rows(conv_in, ALL_ROWS, recv.at[3])
+    with jax.named_scope("back"):
+        lax.fori_loop(0, OWNED, back_body, 0)
+    with jax.named_scope("send_back"):
+        send_all(back, back_in, send.at[4], recv.at[4])
+        send_same(corr, corr_in, send.at[5], recv.at[5], FAR_FIRST)
+
+    with jax.named_scope("wait_conv"):
+        wait_rows(conv_in, ALL_ROWS, recv.at[3])
 
     def query_body(j, carry):
         cols = pl.ds(pl.multiple_of(j * BLOCK, BLOCK), BLOCK)
@@ -313,8 +351,10 @@
         grad_query[0, :, cols] = (out[:, cols].astype(F32) * full).astype(BF16)
         return carry
 
-    lax.fori_loop(0, WIDTH // BLOCK, query_body, 0)
-    wait_rows(back_in, ALL_ROWS, recv.at[4])
+    with jax.named_scope("query_out"):
+        lax.fori_loop(0, WIDTH // BLOCK, query_body, 0)
+    with jax.named_scope("wait_back"):
+        wait_rows(back_in, ALL_ROWS, recv.at[4])
 
     def back_out(j, carry):
         cols = pl.ds(pl.multiple_of(j * BLOCK, BLOCK), BLOCK)
@@ -324,15 +364,11 @@
         grad_value[0, :, cols] = (full * key[:, cols].astype(F32)).astype(BF16)
         return carry
 
-    lax.fori_loop(0, WIDTH // BLOCK, back_out, 0)
-    wait_rows(corr_in, SAME_ROWS, recv.at[5])
-
-    def filter_out(j, carry):
-        cols = pl.ds(pl.multiple_of(j * BLOCK, BLOCK), BLOCK)
-        grad_filter[:, cols] = corr_in[cols, :].T
-        return carry
-
-    lax.fori_loop(0, HALF // BLOCK, filter_out, 0)
+    with jax.named_scope("back_out"):
+        lax.fori_loop(0, WIDTH // BLOCK, back_out, 0)
+    with jax.named_scope("wait_corr"):
+        wait_rows(corr_in, SAME_ROWS, recv.at[5])
+
     wait_rows(mixed_t, ALL_ROWS, send.at[0])
     wait_rows(taps_t, SAME_ROWS, send.at[1])
     wait_rows(gated_t, ALL_ROWS, send.at[2])
@@ -341,48 +377,76 @@
     wait_rows(corr, SAME_ROWS, send.at[5])
 
 
+def in_hbm(x):
+    return pltpu.with_memory_space_constraint(x, pltpu.HBM)
+
+
+def store_kernel(query, key, value, corr, to_query, to_key, to_value, to_filter, flipped, sems):
+    pairs = ((query, to_query), (key, to_key), (value, to_value), (flipped, to_filter))
+    copies = [pltpu.make_async_copy(*pair, sems.at[i]) for i, pair in enumerate(pairs)]
+    for copy in copies[:3]:
+        copy.start()
+    for j in range(HALF // BLOCK):
+        cols = slice(j * BLOCK, (j + 1) * BLOCK)
+        flipped[:, cols] = corr[cols, :].T
+    copies[3].start()
+    for copy in copies:
+        copy.wait()
+
+
 def shards(query_gate, key_input, value_input, grad_output, filter_raw, skip_gain):
     tab, mid = tables()
-    anywhere = pl.BlockSpec(memory_space=pl.ANY)
+    anywhere = pl.BlockSpec(memory_space=pltpu.HBM)
     vmem = pl.BlockSpec(memory_space=pltpu.VMEM)
-    signal = jax.ShapeDtypeStruct((1, BLOCK, WIDTH), BF16)
+    signal = pltpu.VMEM((1, BLOCK, WIDTH), BF16)
     narrow = pltpu.VMEM((BLOCK, WIDTH), BF16)
     tall = pltpu.VMEM((WIDTH, BLOCK), F32)
     short = pltpu.VMEM((HALF, BLOCK), F32)
-    return tuple(
+    gain = skip_gain.reshape(1, WIDTH)
+    arrays = (query_gate, key_input, value_input, grad_output, filter_raw, gain, tab, mid)
+    operands = [in_hbm(x) for x in arrays]
+    results = tuple(
         pl.pallas_call(
             kernel,
-            out_shape=[signal, signal, signal, jax.ShapeDtypeStruct((BLOCK, HALF), F32)],
-            in_specs=[anywhere] * 5 + [vmem] + [anywhere] * 2,
+            out_shape=[signal, signal, signal, pltpu.VMEM((HALF, BLOCK), F32)],
+            in_specs=[anywhere] * 8,
             out_specs=[vmem] * 4,
             scratch_shapes=[narrow] * 4
             + [
                 pltpu.VMEM((BLOCK, HALF), BF16),
                 pltpu.VMEM(tab.shape, BF16),
                 pltpu.VMEM(mid.shape, F32),
+                pltpu.VMEM((1, WIDTH), F32),
             ]
-            + [tall, tall, short] * 4
+            + [tall, tall, short] * 3
+            + [tall, tall]
             + [
                 pltpu.VMEM((OWNED, 2, 2, BLOCK, BLOCK), F32),
                 pltpu.VMEM((OWNED, 2, BLOCK, BLOCK), F32),
-                pltpu.SemaphoreType.DMA((7,)),
+                pltpu.SemaphoreType.DMA((8,)),
                 pltpu.SemaphoreType.DMA((6,)),
                 pltpu.SemaphoreType.DMA((6,)),
             ],
             compiler_params=pltpu.CompilerParams(
-                collective_id=0, has_side_effects=True, vmem_limit_bytes=60 * 1024 * 1024
+                collective_id=0, has_side_effects=True, vmem_limit_bytes=32 * 1024 * 1024
             ),
             name="hyena_back",
-        )(
-            query_gate,
-            key_input,
-            value_input,
-            grad_output,
-            filter_raw,
-            skip_gain.reshape(1, WIDTH),
-            tab,
-            mid,
-        )
+        )(*operands)
+    )
+    return tuple(
+        pl.pallas_call(
+            store_kernel,
+            out_shape=[jax.ShapeDtypeStruct(r.shape, r.dtype) for r in results[:3]]
+            + [jax.ShapeDtypeStruct((BLOCK, HALF), F32)],
+            in_specs=[vmem] * 4,
+            out_specs=[anywhere] * 4,
+            scratch_shapes=[
+                pltpu.VMEM((BLOCK, HALF), F32),
+                pltpu.SemaphoreType.DMA((4,)),
+            ],
+            compiler_params=pltpu.CompilerParams(vmem_limit_bytes=4 * 1024 * 1024),
+            name="store",
+        )(*results)
     )
 
 

time: 146 us -> 133 us (0.911)
  Pallas kernels: 140 us -> 133 us
  local copies, waits for them, and re-layouts: 5.19 us -> 0 us
    pallas_call x1 -> x2, Pallas kernels: 140 us -> 133 us  [the longest x1 131 us: shards(): pl.pallas_call(kernel, out_shape=[signal, signal, signal, pltpu.VMEM((HAL...]
    unnamed x10 -> x0, local copies, waits for them, and re-layouts: 5.19 us -> none
where the time goes in v3:
time: 133 us
  Pallas kernels  133 us (100%)
    pallas_call x1, Pallas kernels, shards(): pl.pallas_call(kernel, out_shape=[signal, signal, signal, pltpu.VMEM((HAL...  131 us

profile of v3, /device:TPU:1, one launch (start us, length us, event | category | flops | bytes accessed | tf_op | source)
XLA Modules:
  0.0 133.3 jit_solution(12789712749631483852)
XLA Ops:
  0.6 131.3 %hyena_back.1 = (bf16[1,128,2048]{2,1,0:T(8,128)(2,1)S(1)}, bf16[1,128,2048]{2,1,0:T(8,128)(2,1)S(1)}, bf16[1,128,2048]{2,1,0:T(8,128)(2,1)S(1)}, f32[1024,128]{1,0:T(8,128)S(1)}) custom-call(bf16[1,128,2048]{2,1,0:T(8,128)(2,1)} %query_hbm.1, bf16[1,128,2048]{2,1,0:T(8,128)(2,1)} %key_hbm.1, bf16[1,128,2048]{2,1,0:T(8,128)(2,1)} %value_hbm.1, ...), custom_call_target="tpu_custom_call" | custom-call | tf_op jit(solution)/shard_map/hyena_back/pallas_call | solution.py:409
  132.0 1.3 %store.1 = (bf16[1,128,2048]{2,1,0:T(8,128)(2,1)}, bf16[1,128,2048]{2,1,0:T(8,128)(2,1)}, bf16[1,128,2048]{2,1,0:T(8,128)(2,1)}, f32[128,1024]{1,0:T(8,128)}) custom-call(bf16[1,128,2048]{2,1,0:T(8,128)(2,1)S(1)} %get-tuple-element.8.query, bf16[1,128,2048]{2,1,0:T(8,128)(2,1)S(1)} %get-tuple-element.9.key, ...), custom_call_target="tpu_custom_call" | custom-call | tf_op jit(solution)/shard_map/store/pallas_call | solution.py:437

commit v4 on v3

--- a/solution.py
+++ b/solution.py
@@ -1,3 +1,4 @@
+import itertools
 import math
 
 import jax
@@ -105,50 +106,56 @@
 
 TURNS = (0, 1, 7, 2, 6, 3, 5, 4)
 SLAB = BLOCK // 8
-FAR_FIRST = ((4, 0), (3, 5), (2, 6), (1, 7))
-
-
-def for_each_peer(visit, turns=TURNS):
-    seq, ch = lax.axis_index("seq"), lax.axis_index("ch")
-    z = lax.div(seq, SLAB)
-    place = lax.rem(seq, SLAB) * 2 + ch
-    bases = [lax.rem(z + turn, 8) * SLAB for turn in turns]
-
-    def at(rest, chosen):
-        low, to_ch = lax.div(rest, 2), lax.rem(rest, 2)
-        for base in chosen:
+
+
+def ring_bases(turns=TURNS):
+    z = lax.div(lax.axis_index("seq"), SLAB)
+    return [lax.rem(z + turn, 8) * SLAB for turn in turns]
+
+
+def at_step(step):
+    place = lax.rem(lax.axis_index("seq"), SLAB) * 2 + lax.axis_index("ch")
+    rest = lax.rem(place + step, 2 * SLAB)
+    return (lax.div(rest, 2), lax.rem(rest, 2))
+
+
+def for_each_peer(visit):
+    bases = ring_bases()
+
+    def body(step, carry):
+        low, to_ch = at_step(step)
+        for base in bases:
             visit(base + low, to_ch)
-
-    def body(step, carry):
-        at(lax.rem(place + step, 2 * SLAB), bases)
-        return carry
-
-    at(place, [base for base, turn in zip(bases, turns) if turn])
+        return carry
+
+    low, to_ch = at_step(0)
+    for base in bases[1:]:
+        visit(base + low, to_ch)
     lax.fori_loop(1, 2 * SLAB, body, 0)
 
 
-def for_each_same(visit, groups=(TURNS,)):
+def hops(move):
+    z, x, y, core = move
+    return (min(z, 8 - z) + 2 * x + min(y, 4 - y), core)
+
+
+MOVES = sorted(itertools.product(range(8), range(2), range(4), range(2)), key=hops)[:0:-1]
+
+
+def for_each_same(visit):
     seq = lax.axis_index("seq")
-    z = lax.div(seq, SLAB)
-    place = lax.rem(seq, SLAB)
-    for turns in groups:
-        bases = [lax.rem(z + turn, 8) * SLAB for turn in turns]
-
-        def body(step, carry, bases=bases):
-            low = lax.rem(place + step, SLAB)
-            for base in bases:
-                visit(base + low)
-            return carry
-
-        for base, turn in zip(bases, turns):
-            if turn:
-                visit(base + place)
-        lax.fori_loop(1, SLAB, body, 0)
-
-
-def send_all(source, target, send, recv):
-    seq, ch = lax.axis_index("seq"), lax.axis_index("ch")
-    me = ch * BLOCK + seq
+    z, x = lax.div(seq, SLAB), lax.rem(lax.div(seq, 8), 2)
+    y, core = lax.rem(lax.div(seq, 2), 4), lax.rem(seq, 2)
+    zs = [lax.rem(z + i, 8) * SLAB for i in range(8)]
+    xs = [lax.rem(x + i, 2) * 8 for i in range(2)]
+    ys = [lax.rem(y + i, 4) * 2 for i in range(4)]
+    cores = [core, 1 - core]
+    for move in MOVES:
+        visit(zs[move[0]] + xs[move[1]] + ys[move[2]] + cores[move[3]])
+
+
+def tile_sender(source, target, send, recv):
+    me = lax.axis_index("ch") * BLOCK + lax.axis_index("seq")
 
     def visit(to_seq, to_ch):
         pltpu.make_async_remote_copy(
@@ -160,11 +167,20 @@
             device_id_type=MESH,
         ).start()
 
-    for_each_peer(visit)
+    return visit
+
+
+def keep_own(source, target):
+    me = lax.axis_index("ch") * BLOCK + lax.axis_index("seq")
     target[tile(me), :] = source[tile(me), :]
 
 
-def send_same(source, target, send, recv, groups=(TURNS,)):
+def send_all(source, target, send, recv):
+    for_each_peer(tile_sender(source, target, send, recv))
+    keep_own(source, target)
+
+
+def send_same(source, target, send, recv):
     seq, ch = lax.axis_index("seq"), lax.axis_index("ch")
 
     def visit(to_seq):
@@ -177,7 +193,7 @@
             device_id_type=MESH,
         ).start()
 
-    for_each_same(visit, groups)
+    for_each_same(visit)
     target[tile(seq), :] = source[tile(seq), :]
 
 
@@ -227,68 +243,113 @@
     load,
     send,
     recv,
+    ready,
 ):
     seq, ch = lax.axis_index("seq"), lax.axis_index("ch")
     barrier = pltpu.get_barrier_semaphore()
 
+    def own_half(ref):
+        return ref.at[:, pl.ds(pl.multiple_of(ch * HALF, HALF), HALF)]
+
+    def other_half(ref):
+        return ref.at[:, pl.ds(pl.multiple_of((1 - ch) * HALF, HALF), HALF)]
+
+    key_src, value_src = key_hbm.at[0], value_hbm.at[0]
     loads = [
-        pltpu.make_async_copy(key_hbm.at[0], key, load.at[0]),
-        pltpu.make_async_copy(value_hbm.at[0], value, load.at[1]),
-        pltpu.make_async_copy(
-            filter_hbm.at[:, pl.ds(pl.multiple_of(ch * HALF, HALF), HALF)], taps, load.at[2]
-        ),
-        pltpu.make_async_copy(out_hbm.at[0], out, load.at[3]),
-        pltpu.make_async_copy(query_hbm.at[0], query, load.at[4]),
-        pltpu.make_async_copy(tab_hbm, tab_ref, load.at[5]),
-        pltpu.make_async_copy(mid_hbm, mid_ref, load.at[6]),
-        pltpu.make_async_copy(gain_hbm, gain_ref, load.at[7]),
+        pltpu.make_async_copy(own_half(key_src), own_half(key), load.at[0]),
+        pltpu.make_async_copy(own_half(value_src), own_half(value), load.at[1]),
+        pltpu.make_async_copy(other_half(key_src), other_half(key), load.at[2]),
+        pltpu.make_async_copy(other_half(value_src), other_half(value), load.at[3]),
+        pltpu.make_async_copy(own_half(filter_hbm), taps, load.at[4]),
+        pltpu.make_async_copy(out_hbm.at[0], out, load.at[5]),
+        pltpu.make_async_copy(query_hbm.at[0], query, load.at[6]),
+        pltpu.make_async_copy(tab_hbm, tab_ref, load.at[7]),
+        pltpu.make_async_copy(mid_hbm, mid_ref, load.at[8]),
+        pltpu.make_async_copy(gain_hbm, gain_ref, load.at[9]),
     ]
-    for copy in loads:
+    for copy in loads[:4]:
         copy.start()
+
+    bases = ring_bases()
 
     def greet(to_seq, to_ch):
         pl.semaphore_signal(barrier, inc=1, device_id=(to_seq, to_ch), device_id_type=MESH)
 
     with jax.named_scope("greet"):
-        for_each_peer(greet, TURNS[::-1])
-
-    def flip_product(left, right, target):
+        for base in bases[:0:-1]:
+            greet(base + lax.rem(seq, SLAB), ch)
+        for step in range(2 * SLAB - 1, 0, -1):
+            low, to_ch = at_step(step)
+            greet(bases[0] + low, to_ch)
+        for copy in loads[4:]:
+            copy.start()
+
+    def flip_product(left, right, target, first=0, count=WIDTH // BLOCK):
         def body(j, carry):
-            cols = pl.ds(pl.multiple_of(j * BLOCK, BLOCK), BLOCK)
+            cols = pl.ds(pl.multiple_of(first + j * BLOCK, BLOCK), BLOCK)
             target[cols, :] = (left[:, cols].astype(F32) * right[:, cols].astype(F32)).T
             return carry
 
-        lax.fori_loop(0, WIDTH // BLOCK, body, 0)
-
+        lax.fori_loop(0, count, body, 0)
+
+    def flip_taps(j, carry):
+        cols = pl.ds(pl.multiple_of(j * BLOCK, BLOCK), BLOCK)
+        taps_t[cols, :] = taps[:, cols].astype(F32).T
+        return carry
+
+    send_mixed = tile_sender(mixed_t, mixed_in, send.at[0], recv.at[0])
+
+    def mixed_step(step):
+        low, to_ch = at_step(step)
+        pl.semaphore_wait(ready.at[2 * low + to_ch], 1)
+        for base in bases:
+            send_mixed(base + low, to_ch)
+
+    def mixed_even(i, carry):
+        mixed_step(2 * i)
+        return carry
+
+    def mixed_odd(i, carry):
+        mixed_step(2 * i + 1)
+        return carry
+
+    with jax.named_scope("barrier"):
+        pl.semaphore_wait(barrier, 7 + 2 * SLAB - 1)
+        mine = ready.at[2 * lax.rem(seq, SLAB) + ch]
+        for step in range(1, 2 * SLAB):
+            low, to_ch = at_step(step)
+            pl.semaphore_signal(
+                mine, inc=1, device_id=(bases[0] + low, to_ch), device_id_type=MESH
+            )
     with jax.named_scope("load"):
         loads[0].wait()
         loads[1].wait()
     with jax.named_scope("flip_mixed"):
-        flip_product(key, value, mixed_t)
-    loads[2].wait()
-
-    def flip_taps(j, carry):
-        cols = pl.ds(pl.multiple_of(j * BLOCK, BLOCK), BLOCK)
-        taps_t[cols, :] = taps[:, cols].astype(F32).T
-        return carry
-
+        flip_product(key, value, mixed_t, ch * HALF, HALF // BLOCK)
+    with jax.named_scope("send_mixed"):
+        for base in bases[1:]:
+            send_mixed(base + lax.rem(seq, SLAB), ch)
+        lax.fori_loop(1, SLAB, mixed_even, 0)
+    with jax.named_scope("flip_mixed2"):
+        loads[2].wait()
+        loads[3].wait()
+        flip_product(key, value, mixed_t, (1 - ch) * HALF, HALF // BLOCK)
+    with jax.named_scope("send_mixed2"):
+        lax.fori_loop(0, SLAB, mixed_odd, 0)
+        keep_own(mixed_t, mixed_in)
     with jax.named_scope("flip_taps"):
+        loads[4].wait()
         lax.fori_loop(0, HALF // BLOCK, flip_taps, 0)
-    with jax.named_scope("barrier"):
-        pl.semaphore_wait(barrier, 2 * BLOCK - 1)
-    with jax.named_scope("send_mixed"):
-        send_all(mixed_t, mixed_in, send.at[0], recv.at[0])
     with jax.named_scope("send_taps"):
         send_same(taps_t, taps_in, send.at[1], recv.at[1])
-    loads[3].wait()
-    loads[4].wait()
+    loads[5].wait()
+    loads[6].wait()
     with jax.named_scope("flip_gated"):
         flip_product(out, query, gated_t)
     with jax.named_scope("send_gated"):
         send_all(gated_t, gated_in, send.at[2], recv.at[2])
-    loads[5].wait()
-    loads[6].wait()
-    loads[7].wait()
+    for copy in loads[7:]:
+        copy.wait()
     with jax.named_scope("wait_mixed"):
         wait_rows(mixed_in, ALL_ROWS, recv.at[0])
         wait_rows(taps_in, SAME_ROWS, recv.at[1])
@@ -339,7 +400,7 @@
         lax.fori_loop(0, OWNED, back_body, 0)
     with jax.named_scope("send_back"):
         send_all(back, back_in, send.at[4], recv.at[4])
-        send_same(corr, corr_in, send.at[5], recv.at[5], FAR_FIRST)
+        send_same(corr, corr_in, send.at[5], recv.at[5])
 
     with jax.named_scope("wait_conv"):
         wait_rows(conv_in, ALL_ROWS, recv.at[3])
@@ -368,7 +429,6 @@
         lax.fori_loop(0, WIDTH // BLOCK, back_out, 0)
     with jax.named_scope("wait_corr"):
         wait_rows(corr_in, SAME_ROWS, recv.at[5])
-
     wait_rows(mixed_t, ALL_ROWS, send.at[0])
     wait_rows(taps_t, SAME_ROWS, send.at[1])
     wait_rows(gated_t, ALL_ROWS, send.at[2])
@@ -423,9 +483,10 @@
             + [
                 pltpu.VMEM((OWNED, 2, 2, BLOCK, BLOCK), F32),
                 pltpu.VMEM((OWNED, 2, BLOCK, BLOCK), F32),
-                pltpu.SemaphoreType.DMA((8,)),
+                pltpu.SemaphoreType.DMA((10,)),
                 pltpu.SemaphoreType.DMA((6,)),
                 pltpu.SemaphoreType.DMA((6,)),
+                pltpu.SemaphoreType.REGULAR((2 * SLAB,)),
             ],
             compiler_params=pltpu.CompilerParams(
                 collective_id=0, has_side_effects=True, vmem_limit_bytes=32 * 1024 * 1024

time: 133 us -> 131 us (0.985)
  Pallas kernels: 133 us -> 130 us
    pallas_call x1, Pallas kernels: 131 us -> 129 us  [shards(): pl.pallas_call(kernel, out_shape=[signal, signal, signal, pltpu.VMEM((HAL...]
where the time goes in v4:
time: 131 us
  Pallas kernels  130 us (99%)
    pallas_call x1, Pallas kernels, shards(): pl.pallas_call(kernel, out_shape=[signal, signal, signal, pltpu.VMEM((HAL...  129 us

profile of v4, /device:TPU:1, one launch (start us, length us, event | category | flops | bytes accessed | tf_op | source)
XLA Modules:
  0.0 130.9 jit_solution(9934613878723110523)
XLA Ops:
  0.6 128.9 %hyena_back.1 = (bf16[1,128,2048]{2,1,0:T(8,128)(2,1)S(1)}, bf16[1,128,2048]{2,1,0:T(8,128)(2,1)S(1)}, bf16[1,128,2048]{2,1,0:T(8,128)(2,1)S(1)}, f32[1024,128]{1,0:T(8,128)S(1)}) custom-call(bf16[1,128,2048]{2,1,0:T(8,128)(2,1)} %query_hbm.1, bf16[1,128,2048]{2,1,0:T(8,128)(2,1)} %key_hbm.1, bf16[1,128,2048]{2,1,0:T(8,128)(2,1)} %value_hbm.1, ...), custom_call_target="tpu_custom_call" | custom-call | tf_op jit(solution)/shard_map/hyena_back/pallas_call | solution.py:469
  129.5 1.3 %store.1 = (bf16[1,128,2048]{2,1,0:T(8,128)(2,1)}, bf16[1,128,2048]{2,1,0:T(8,128)(2,1)}, bf16[1,128,2048]{2,1,0:T(8,128)(2,1)}, f32[128,1024]{1,0:T(8,128)}) custom-call(bf16[1,128,2048]{2,1,0:T(8,128)(2,1)S(1)} %get-tuple-element.8.query, bf16[1,128,2048]{2,1,0:T(8,128)(2,1)S(1)} %get-tuple-element.9.key, ...), custom_call_target="tpu_custom_call" | custom-call | tf_op jit(solution)/shard_map/store/pallas_call | solution.py:498

commit v5 on v4

--- a/solution.py
+++ b/solution.py
@@ -136,10 +136,31 @@
 
 def hops(move):
     z, x, y, core = move
-    return (min(z, 8 - z) + 2 * x + min(y, 4 - y), core)
+    return (2 * x + min(y, 4 - y) + core, min(z, 8 - z))
 
 
 MOVES = sorted(itertools.product(range(8), range(2), range(4), range(2)), key=hops)[:0:-1]
+
+
+def hops_all(move):
+    z, x, y, core = move
+    return (min(x, 4 - x) + min(y, 4 - y) + core, min(z, 8 - z))
+
+
+MOVES_ALL = sorted(itertools.product(range(8), range(4), range(4), range(2)), key=hops_all)[:0:-1]
+
+
+def for_each_far(visit):
+    seq, ch = lax.axis_index("seq"), lax.axis_index("ch")
+    z, x = lax.div(seq, SLAB), lax.rem(lax.div(seq, 8), 2) * 2 + ch
+    y, core = lax.rem(lax.div(seq, 2), 4), lax.rem(seq, 2)
+    zs = [lax.rem(z + i, 8) * SLAB for i in range(8)]
+    xs = [lax.rem(x + i, 4) for i in range(4)]
+    highs, lows = [lax.div(i, 2) * 8 for i in xs], [lax.rem(i, 2) for i in xs]
+    ys = [lax.rem(y + i, 4) * 2 for i in range(4)]
+    cores = [core, 1 - core]
+    for move in MOVES_ALL:
+        visit(zs[move[0]] + highs[move[1]] + ys[move[2]] + cores[move[3]], lows[move[1]])
 
 
 def for_each_same(visit):
@@ -175,8 +196,8 @@
     target[tile(me), :] = source[tile(me), :]
 
 
-def send_all(source, target, send, recv):
-    for_each_peer(tile_sender(source, target, send, recv))
+def send_all(source, target, send, recv, visits=None):
+    (visits or for_each_peer)(tile_sender(source, target, send, recv))
     keep_own(source, target)
 
 
@@ -399,7 +420,7 @@
     with jax.named_scope("back"):
         lax.fori_loop(0, OWNED, back_body, 0)
     with jax.named_scope("send_back"):
-        send_all(back, back_in, send.at[4], recv.at[4])
+        send_all(back, back_in, send.at[4], recv.at[4], for_each_far)
         send_same(corr, corr_in, send.at[5], recv.at[5])
 
     with jax.named_scope("wait_conv"):
@@ -442,14 +463,20 @@
 
 
 def store_kernel(query, key, value, corr, to_query, to_key, to_value, to_filter, flipped, sems):
-    pairs = ((query, to_query), (key, to_key), (value, to_value), (flipped, to_filter))
-    copies = [pltpu.make_async_copy(*pair, sems.at[i]) for i, pair in enumerate(pairs)]
-    for copy in copies[:3]:
+    copies = [
+        pltpu.make_async_copy(*pair, sems.at[i])
+        for i, pair in enumerate(((query, to_query), (key, to_key), (value, to_value)))
+    ]
+    for copy in copies:
         copy.start()
-    for j in range(HALF // BLOCK):
-        cols = slice(j * BLOCK, (j + 1) * BLOCK)
-        flipped[:, cols] = corr[cols, :].T
-    copies[3].start()
+    for i in range(4):
+        for j in range(2 * i, 2 * i + 2):
+            cols = slice(j * BLOCK, (j + 1) * BLOCK)
+            flipped[:, cols] = corr[cols, :].T
+        cols = pl.ds(2 * i * BLOCK, 2 * BLOCK)
+        copy = pltpu.make_async_copy(flipped.at[:, cols], to_filter.at[:, cols], sems.at[3 + i])
+        copy.start()
+        copies.append(copy)
     for copy in copies:
         copy.wait()
 
@@ -503,7 +530,7 @@
             out_specs=[anywhere] * 4,
             scratch_shapes=[
                 pltpu.VMEM((BLOCK, HALF), F32),
-                pltpu.SemaphoreType.DMA((4,)),
+                pltpu.SemaphoreType.DMA((7,)),
             ],
             compiler_params=pltpu.CompilerParams(vmem_limit_bytes=4 * 1024 * 1024),
             name="store",

time: 131 us -> 130 us (level)
  no operation moved by 1% of the time
where the time goes in v5:
time: 130 us
  Pallas kernels  130 us (100%)
    pallas_call x1, Pallas kernels, shards(): pl.pallas_call(kernel, out_shape=[signal, signal, signal, pltpu.VMEM((HAL...  128 us

profile of v5, /device:TPU:1, one launch (start us, length us, event | category | flops | bytes accessed | tf_op | source)
XLA Modules:
  0.0 130.2 jit_solution(13751360951686767711)
XLA Ops:
  0.6 128.2 %hyena_back.1 = (bf16[1,128,2048]{2,1,0:T(8,128)(2,1)S(1)}, bf16[1,128,2048]{2,1,0:T(8,128)(2,1)S(1)}, bf16[1,128,2048]{2,1,0:T(8,128)(2,1)S(1)}, f32[1024,128]{1,0:T(8,128)S(1)}) custom-call(bf16[1,128,2048]{2,1,0:T(8,128)(2,1)} %query_hbm.1, bf16[1,128,2048]{2,1,0:T(8,128)(2,1)} %key_hbm.1, bf16[1,128,2048]{2,1,0:T(8,128)(2,1)} %value_hbm.1, ...), custom_call_target="tpu_custom_call" | custom-call | tf_op jit(solution)/shard_map/hyena_back/pallas_call | solution.py:496
  128.8 1.4 %store.1 = (bf16[1,128,2048]{2,1,0:T(8,128)(2,1)}, bf16[1,128,2048]{2,1,0:T(8,128)(2,1)}, bf16[1,128,2048]{2,1,0:T(8,128)(2,1)}, f32[128,1024]{1,0:T(8,128)}) custom-call(bf16[1,128,2048]{2,1,0:T(8,128)(2,1)S(1)} %get-tuple-element.8.query, bf16[1,128,2048]{2,1,0:T(8,128)(2,1)S(1)} %get-tuple-element.9.key, ...), custom_call_target="tpu_custom_call" | custom-call | tf_op jit(solution)/shard_map/store/pallas_call | solution.py:525

commit v6 on v5

--- a/solution.py
+++ b/solution.py
@@ -117,6 +117,25 @@
     place = lax.rem(lax.axis_index("seq"), SLAB) * 2 + lax.axis_index("ch")
     rest = lax.rem(place + step, 2 * SLAB)
     return (lax.div(rest, 2), lax.rem(rest, 2))
+
+
+def hops_plane(move):
+    x, y, core = move
+    return (min(x, 4 - x) + min(y, 4 - y), core)
+
+
+PLANE = sorted(itertools.product(range(4), range(4), range(2)), key=hops_plane)[1:]
+NEAR_FIRST = ([move for move in PLANE if move[0] % 2 == 0], [move for move in PLANE if move[0] % 2])
+
+
+def slab_places(moves):
+    seq, ch = lax.axis_index("seq"), lax.axis_index("ch")
+    x, y = lax.rem(lax.div(seq, 8), 2) * 2 + ch, lax.rem(lax.div(seq, 2), 4)
+    cores = [lax.rem(seq, 2), 1 - lax.rem(seq, 2)]
+    xs = [lax.rem(x + i, 4) for i in range(4)]
+    highs, lows = [lax.div(i, 2) * 8 for i in xs], [lax.rem(i, 2) for i in xs]
+    ys = [lax.rem(y + i, 4) * 2 for i in range(4)]
+    return [(highs[dx] + ys[dy] + cores[dcore], lows[dx]) for dx, dy, dcore in moves]
 
 
 def for_each_peer(visit):
@@ -299,8 +318,7 @@
     with jax.named_scope("greet"):
         for base in bases[:0:-1]:
             greet(base + lax.rem(seq, SLAB), ch)
-        for step in range(2 * SLAB - 1, 0, -1):
-            low, to_ch = at_step(step)
+        for low, to_ch in slab_places(PLANE[::-1]):
             greet(bases[0] + low, to_ch)
         for copy in loads[4:]:
             copy.start()
@@ -320,25 +338,16 @@
 
     send_mixed = tile_sender(mixed_t, mixed_in, send.at[0], recv.at[0])
 
-    def mixed_step(step):
-        low, to_ch = at_step(step)
-        pl.semaphore_wait(ready.at[2 * low + to_ch], 1)
-        for base in bases:
-            send_mixed(base + low, to_ch)
-
-    def mixed_even(i, carry):
-        mixed_step(2 * i)
-        return carry
-
-    def mixed_odd(i, carry):
-        mixed_step(2 * i + 1)
-        return carry
+    def mixed_steps(moves):
+        for low, to_ch in slab_places(moves):
+            pl.semaphore_wait(ready.at[2 * low + to_ch], 1)
+            for base in bases:
+                send_mixed(base + low, to_ch)
 
     with jax.named_scope("barrier"):
         pl.semaphore_wait(barrier, 7 + 2 * SLAB - 1)
         mine = ready.at[2 * lax.rem(seq, SLAB) + ch]
-        for step in range(1, 2 * SLAB):
-            low, to_ch = at_step(step)
+        for low, to_ch in slab_places(PLANE[::-1]):
             pl.semaphore_signal(
                 mine, inc=1, device_id=(bases[0] + low, to_ch), device_id_type=MESH
             )
@@ -350,13 +359,13 @@
     with jax.named_scope("send_mixed"):
         for base in bases[1:]:
             send_mixed(base + lax.rem(seq, SLAB), ch)
-        lax.fori_loop(1, SLAB, mixed_even, 0)
+        mixed_steps(NEAR_FIRST[0])
     with jax.named_scope("flip_mixed2"):
         loads[2].wait()
         loads[3].wait()
         flip_product(key, value, mixed_t, (1 - ch) * HALF, HALF // BLOCK)
     with jax.named_scope("send_mixed2"):
-        lax.fori_loop(0, SLAB, mixed_odd, 0)
+        mixed_steps(NEAR_FIRST[1])
         keep_own(mixed_t, mixed_in)
     with jax.named_scope("flip_taps"):
         loads[4].wait()
@@ -368,7 +377,7 @@
     with jax.named_scope("flip_gated"):
         flip_product(out, query, gated_t)
     with jax.named_scope("send_gated"):
-        send_all(gated_t, gated_in, send.at[2], recv.at[2])
+        send_all(gated_t, gated_in, send.at[2], recv.at[2], for_each_far)
     for copy in loads[7:]:
         copy.wait()
     with jax.named_scope("wait_mixed"):
@@ -396,7 +405,7 @@
     with jax.named_scope("conv"):
         lax.fori_loop(0, OWNED, conv_body, 0)
     with jax.named_scope("send_conv"):
-        send_all(conv, conv_in, send.at[3], recv.at[3])
+        send_all(conv, conv_in, send.at[3], recv.at[3], for_each_far)
     with jax.named_scope("wait_gated"):
         wait_rows(gated_in, ALL_ROWS, recv.at[2])
 

time: 130 us -> 130 us (level)
  no operation moved by 1% of the time
where the time goes in v6:
time: 130 us
  Pallas kernels  129 us (99%)
    pallas_call x1, Pallas kernels, shards(): pl.pallas_call(kernel, out_shape=[signal, signal, signal, pltpu.VMEM((HAL...  128 us

profile of v6, /device:TPU:1, one launch (start us, length us, event | category | flops | bytes accessed | tf_op | source)
XLA Modules:
  0.0 130.0 jit_solution(13372981746720438651)
XLA Ops:
  0.6 128.0 %hyena_back.1 = (bf16[1,128,2048]{2,1,0:T(8,128)(2,1)S(1)}, bf16[1,128,2048]{2,1,0:T(8,128)(2,1)S(1)}, bf16[1,128,2048]{2,1,0:T(8,128)(2,1)S(1)}, f32[1024,128]{1,0:T(8,128)S(1)}) custom-call(bf16[1,128,2048]{2,1,0:T(8,128)(2,1)} %query_hbm.1, bf16[1,128,2048]{2,1,0:T(8,128)(2,1)} %key_hbm.1, bf16[1,128,2048]{2,1,0:T(8,128)(2,1)} %value_hbm.1, ...), custom_call_target="tpu_custom_call" | custom-call | tf_op jit(solution)/shard_map/hyena_back/pallas_call | solution.py:505
  128.6 1.4 %store.1 = (bf16[1,128,2048]{2,1,0:T(8,128)(2,1)}, bf16[1,128,2048]{2,1,0:T(8,128)(2,1)}, bf16[1,128,2048]{2,1,0:T(8,128)(2,1)}, f32[128,1024]{1,0:T(8,128)}) custom-call(bf16[1,128,2048]{2,1,0:T(8,128)(2,1)S(1)} %get-tuple-element.8.query, bf16[1,128,2048]{2,1,0:T(8,128)(2,1)S(1)} %get-tuple-element.9.key, ...), custom_call_target="tpu_custom_call" | custom-call | tf_op jit(solution)/shard_map/store/pallas_call | solution.py:534

commit v7 on v6

--- a/solution.py
+++ b/solution.py
@@ -155,18 +155,20 @@
 
 def hops(move):
     z, x, y, core = move
-    return (2 * x + min(y, 4 - y) + core, min(z, 8 - z))
-
-
-MOVES = sorted(itertools.product(range(8), range(2), range(4), range(2)), key=hops)[:0:-1]
+    return (2 * x + min(y, 4 - y) + 1 - core, min(z, 8 - z))
+
+
+MOVES = sorted(itertools.product(range(8), range(2), range(4), range(2)), key=hops)[::-1]
+MOVES = [move for move in MOVES if any(move[:3])]
 
 
 def hops_all(move):
     z, x, y, core = move
-    return (min(x, 4 - x) + min(y, 4 - y) + core, min(z, 8 - z))
-
-
-MOVES_ALL = sorted(itertools.product(range(8), range(4), range(4), range(2)), key=hops_all)[:0:-1]
+    return (min(x, 4 - x) + min(y, 4 - y) + 1 - core, min(z, 8 - z))
+
+
+MOVES_ALL = sorted(itertools.product(range(8), range(4), range(4), range(2)), key=hops_all)[::-1]
+MOVES_ALL = [move for move in MOVES_ALL if any(move[:3])]
 
 
 def for_each_far(visit):
@@ -177,9 +179,9 @@
     xs = [lax.rem(x + i, 4) for i in range(4)]
     highs, lows = [lax.div(i, 2) * 8 for i in xs], [lax.rem(i, 2) for i in xs]
     ys = [lax.rem(y + i, 4) * 2 for i in range(4)]
-    cores = [core, 1 - core]
     for move in MOVES_ALL:
-        visit(zs[move[0]] + highs[move[1]] + ys[move[2]] + cores[move[3]], lows[move[1]])
+        visit(zs[move[0]] + highs[move[1]] + ys[move[2]] + move[3], lows[move[1]])
+    visit(zs[0] + highs[0] + ys[0] + 1 - core, lows[0])
 
 
 def for_each_same(visit):
@@ -189,9 +191,9 @@
     zs = [lax.rem(z + i, 8) * SLAB for i in range(8)]
     xs = [lax.rem(x + i, 2) * 8 for i in range(2)]
     ys = [lax.rem(y + i, 4) * 2 for i in range(4)]
-    cores = [core, 1 - core]
     for move in MOVES:
-        visit(zs[move[0]] + xs[move[1]] + ys[move[2]] + cores[move[3]])
+        visit(zs[move[0]] + xs[move[1]] + ys[move[2]] + move[3])
+    visit(zs[0] + xs[0] + ys[0] + 1 - core)
 
 
 def tile_sender(source, target, send, recv):

time: 130 us -> 130 us (level)
  no operation moved by 1% of the time
where the time goes in v7:
time: 130 us
  Pallas kernels  130 us (100%)
    pallas_call x1, Pallas kernels, shards(): pl.pallas_call(kernel, out_shape=[signal, signal, signal, pltpu.VMEM((HAL...  128 us

profile of v7, /device:TPU:1, one launch (start us, length us, event | category | flops | bytes accessed | tf_op | source)
XLA Modules:
  0.0 130.3 jit_solution(7792347015075507468)
XLA Ops:
  0.6 128.3 %hyena_back.1 = (bf16[1,128,2048]{2,1,0:T(8,128)(2,1)S(1)}, bf16[1,128,2048]{2,1,0:T(8,128)(2,1)S(1)}, bf16[1,128,2048]{2,1,0:T(8,128)(2,1)S(1)}, f32[1024,128]{1,0:T(8,128)S(1)}) custom-call(bf16[1,128,2048]{2,1,0:T(8,128)(2,1)} %query_hbm.1, bf16[1,128,2048]{2,1,0:T(8,128)(2,1)} %key_hbm.1, bf16[1,128,2048]{2,1,0:T(8,128)(2,1)} %value_hbm.1, ...), custom_call_target="tpu_custom_call" | custom-call | tf_op jit(solution)/shard_map/hyena_back/pallas_call | solution.py:507
  129.0 1.4 %store.1 = (bf16[1,128,2048]{2,1,0:T(8,128)(2,1)}, bf16[1,128,2048]{2,1,0:T(8,128)(2,1)}, bf16[1,128,2048]{2,1,0:T(8,128)(2,1)}, f32[128,1024]{1,0:T(8,128)}) custom-call(bf16[1,128,2048]{2,1,0:T(8,128)(2,1)S(1)} %get-tuple-element.8.query, bf16[1,128,2048]{2,1,0:T(8,128)(2,1)S(1)} %get-tuple-element.9.key, ...), custom_call_target="tpu_custom_call" | custom-call | tf_op jit(solution)/shard_map/store/pallas_call | solution.py:536
